TPU v7x, 128 devices: a whole 4x4x4 slice. The times are simulated.
128 devices in a mesh: rep: 16 (over x, y_lo, core), tp: 8 (over z, y_hi).
Axes of the slice: x: 4, y: 4 (y_hi: 2, y_lo: 2; y = y_hi * 2 + y_lo), z: 4, core: 2. Of those that a mesh axis runs over, the one named last changes fastest.
Arguments:
- context: bfloat16 [32768, 5120], P('rep', 'tp'), may hold values from -6 to 6
- out_grad: bfloat16 [32768, 5120], P('rep', 'tp'), may hold values from -6 to 6
- rewards: int32 [8, 64], P(None, 'rep'), may hold values from 0 to 1
- master: float32 [5120, 5120], P('rep', 'tp'), may hold values from -0.078125 to 0.078125
- first_moment: float32 [5120, 5120], P('rep', 'tp'), may hold values from -0.03125 to 0.03125
- second_moment: float32 [5120, 5120], P('rep', 'tp'), may hold values from 3.0517577e-07 to 3.0517578e-05
- inputs: bfloat16 [4, 512, 5120], P(None, 'rep'), may hold values from -6 to 6
- w_query: bfloat16 [5120, 5120], P(None, 'tp'), may hold values from -0.078125 to 0.078125
- w_key: bfloat16 [5120, 1024], P(None, 'tp'), may hold values from -0.078125 to 0.078125
- w_value: bfloat16 [5120, 1024], P(None, 'tp'), may hold values from -0.078125 to 0.078125
- cache_keys: bfloat16 [512, 256, 1024], P('rep', None, 'tp'), may hold values from -400 to 400
- cache_values: bfloat16 [512, 256, 1024], P('rep', None, 'tp'), may hold values from -24 to 24
- lengths: int32 [64], P('rep'), may hold values from 64 to 256
Outputs:
- decoded: bfloat16 [4, 512, 5120], P(None, 'rep')
- adam_step: float32 [5120, 5120], P('rep', 'tp')
All inputs are finite; a program needn't handle non-finite values.
Results may differ from a plain program's by a relative error of at most 0.0088.
Values may be sent and summed in bfloat16 or wider, within the bound.
A program may use at most 128 MiB of HBM per device.

v0:
```python
import jax
import jax.numpy as jnp
from jax import lax
from jax.sharding import PartitionSpec as P

HEAD_DIM = 128


rope_base = 1000000.0
first_beta = 0.9
second_beta = 0.95
adam_epsilon = 1e-08
step_count = 10
learn_rate = 0.001


def from_everyone(array, axis):
    devices = lax.axis_size(axis)
    return lax.all_to_all(
        jnp.broadcast_to(array[None], (devices, *array.shape)), axis, 0, 0, tiled=True
    )


def of_everyone(array, axis):
    everything = from_everyone(array, axis)
    return jnp.sum(everything, axis=0)


def laid_out(tiles, dim):
    tiles = jnp.moveaxis(tiles, 0, dim)
    lengths = tiles.shape
    return tiles.reshape(*lengths[:dim], lengths[dim] * lengths[dim + 1], *lengths[dim + 2 :])


def collect(array, axis, dim):
    return laid_out(from_everyone(array, axis), dim)


def split_up(array, dim, devices):
    before, after = (array.shape[:dim], array.shape[dim + 1 :])
    return jnp.moveaxis(array.reshape(*before, devices, -1, *after), dim, 0)


def sum_at_owner(array, axis, dim):
    tiles = split_up(array, dim, lax.axis_size(axis))
    arrived = lax.all_to_all(tiles, axis, split_axis=0, concat_axis=0, tiled=True)
    return arrived.sum(axis=0)


def rotate(vectors, positions):
    half_dim = vectors.shape[-1] // 2
    frequency = rope_base ** (-2.0 * jnp.arange(half_dim, dtype=jnp.float32) / vectors.shape[-1])
    angles = positions[..., None].astype(jnp.float32) * frequency
    cosine_table = jnp.cos(angles)
    sine_table = jnp.sin(angles)
    former = vectors[..., :half_dim]
    latter = vectors[..., half_dim:]
    return jnp.concatenate(
        [former * cosine_table - latter * sine_table, latter * cosine_table + former * sine_table],
        axis=-1,
    )


def attend(queries, old_keys, old_values, new_keys, new_values, live_mask):
    score_scale = HEAD_DIM ** (-0.5)
    step_total = queries.shape[0]
    cache_scores = (
        jnp.einsum("tsgqd,scgd->tsgqc", queries, old_keys, preferred_element_type=jnp.float32)
        * score_scale
    )
    cache_scores = jnp.where(live_mask[None, :, None, None, :], cache_scores, -1e30)
    recent = (
        jnp.einsum("tsgqd,usgd->tsgqu", queries, new_keys, preferred_element_type=jnp.float32)
        * score_scale
    )
    causal = jnp.arange(step_total)[:, None] >= jnp.arange(step_total)[None, :]
    recent = jnp.where(causal[:, None, None, None, :], recent, -1e30)
    row_peak = jnp.maximum(jnp.max(cache_scores, axis=-1), jnp.max(recent, axis=-1))[..., None]
    cache_exp = jnp.exp(cache_scores - row_peak)
    recent_exp = jnp.exp(recent - row_peak)
    denominator = jnp.sum(cache_exp, axis=-1, keepdims=True) + jnp.sum(
        recent_exp, axis=-1, keepdims=True
    )
    cache_weight = (cache_exp / denominator).astype(jnp.bfloat16)
    recent_weight = (recent_exp / denominator).astype(jnp.bfloat16)
    attended = jnp.einsum(
        "tsgqc,scgd->tsgqd", cache_weight, old_values, preferred_element_type=jnp.float32
    )
    attended = attended + jnp.einsum(
        "tsgqu,usgd->tsgqd", recent_weight, new_values, preferred_element_type=jnp.float32
    )
    return attended.astype(jnp.bfloat16)


def per_device(
    context,
    out_grad,
    rewards,
    master,
    first_moment,
    second_moment,
    inputs,
    w_query,
    w_key,
    w_value,
    cache_keys,
    cache_values,
    lengths,
):
    replicas = lax.axis_size("rep")
    prompt_count, local_group = rewards.shape
    totals = of_everyone(jnp.sum(rewards, axis=1), "rep")
    group_size = local_group * replicas
    advantage = rewards.astype(jnp.float32) - totals.astype(jnp.float32)[:, None] / group_size
    token_local = context.shape[0]
    per_token = jnp.repeat(advantage.reshape(-1), token_local // (prompt_count * local_group)) / (
        token_local * replicas
    )
    scaled = (out_grad.astype(jnp.float32) * per_token[:, None]).astype(jnp.bfloat16)
    features = lax.all_gather(context, "tp", axis=1, tiled=True)
    gradient = lax.psum_scatter(
        lax.dot_general(
            features, scaled, (((0,), (0,)), ((), ())), preferred_element_type=jnp.float32
        ).astype(jnp.bfloat16),
        "rep",
        scatter_dimension=0,
        tiled=True,
    ).astype(jnp.float32)
    moment_new = first_beta * first_moment + (1.0 - first_beta) * gradient
    square_new = second_beta * second_moment + (1.0 - second_beta) * gradient * gradient
    adam_step = (
        moment_new
        / (1.0 - first_beta**step_count)
        / (jnp.sqrt(square_new / (1.0 - second_beta**step_count)) + adam_epsilon)
    )
    weight = (master - learn_rate * adam_step).astype(jnp.bfloat16)
    step_total, seq_local, model_width = inputs.shape
    local_heads = w_query.shape[1] // HEAD_DIM
    local_kv = w_key.shape[1] // HEAD_DIM
    flat_rows = inputs.reshape(step_total * seq_local, model_width)
    queries = jnp.dot(flat_rows, w_query, preferred_element_type=jnp.float32).reshape(
        step_total, seq_local, local_heads, HEAD_DIM
    )
    key_new = jnp.dot(flat_rows, w_key, preferred_element_type=jnp.float32).reshape(
        step_total, seq_local, local_kv, HEAD_DIM
    )
    value_new = (
        jnp.dot(flat_rows, w_value, preferred_element_type=jnp.float32)
        .reshape(step_total, seq_local, local_kv, HEAD_DIM)
        .astype(jnp.bfloat16)
    )
    seq_length = jnp.repeat(lengths, seq_local // lengths.shape[0])
    positions = seq_length[None, :] + jnp.arange(step_total, dtype=jnp.int32)[:, None]
    queries = rotate(queries, positions[:, :, None]).astype(jnp.bfloat16)
    queries = queries.reshape(step_total, seq_local, local_kv, local_heads // local_kv, HEAD_DIM)
    key_new = rotate(key_new, positions[:, :, None]).astype(jnp.bfloat16)
    slot_total = cache_keys.shape[1]
    old_keys = cache_keys.reshape(seq_local, slot_total, local_kv, HEAD_DIM)
    old_values = cache_values.reshape(seq_local, slot_total, local_kv, HEAD_DIM)
    live_mask = jnp.arange(slot_total, dtype=jnp.int32)[None, :] < seq_length[:, None]
    attended = attend(queries, old_keys, old_values, key_new, value_new, live_mask)
    attended = attended.reshape(step_total * seq_local, local_heads * HEAD_DIM)
    all_heads = collect(attended, "tp", 1)
    feature_rows = lax.all_to_all(all_heads, "rep", split_axis=1, concat_axis=0, tiled=True)
    own_columns = sum_at_owner(
        jnp.dot(feature_rows, weight, preferred_element_type=jnp.float32), "rep", 0
    )
    decoded = collect(own_columns.astype(jnp.bfloat16), "tp", 1)
    return (decoded.reshape(step_total, seq_local, model_width), adam_step)


def solution(mesh):
    placed = (
        P("rep", "tp"),
        P("rep", "tp"),
        P(None, "rep"),
        P("rep", "tp"),
        P("rep", "tp"),
        P("rep", "tp"),
        P(None, "rep", None),
        P(None, "tp"),
        P(None, "tp"),
        P(None, "tp"),
        P("rep", None, "tp"),
        P("rep", None, "tp"),
        P("rep"),
    )
    return jax.shard_map(
        per_device,
        mesh=mesh,
        in_specs=placed,
        out_specs=(P(None, "rep", None), P("rep", "tp")),
        check_vma=False,
    )
```

profile of v0, /device:TPU:0, one launch (start us, length us, event | category | flops | bytes accessed | tf_op | source)
XLA Modules:
  0.0 483.4 jit_solution(15974922212269263185)
XLA Ops:
  7.2 0.0 copy-start
  7.2 0.0 copy-start.5
  7.2 0.0 all-gather.2.cloned.1.call-start
  7.2 0.7 all-gather.2.cloned.1.call-update
  7.9 0.0 reduce-scatter.4.cloned.1.call-start
  8.0 0.0 copy-done.5
  8.0 11.4 %all_to_all.37 = s32[16,1,8]{2,1,0:T(1,128)S(1)} all-to-all(s32[16,1,8]{2,1,0:T(1,128)S(1)} %broadcast_in_dim.69), channel_id=1, replica_groups=mesh['rep'=16,'tp'=8] {'rep'}, dimensions={0} | all-to-all | bytes 1024 | tf_op jit(solution)/shard_map/all_to_all | solution.py:19
  19.5 0.1 copy.87
  19.6 0.1 div.61
  19.7 0.1 broadcast_in_dim.70
  19.7 0.1 div.62
  19.8 212.7 %all-gather.2.cloned.1.call-done = bf16[2048,5120]{1,0:T(8,128)(2,1)} async-done(((bf16[2048,640]{1,0:T(8,128)(2,1)}), bf16[2048,5120]{1,0:T(8,128)(2,1)}) %all-gather.2.cloned.1.call-update) | async-done | bytes 20971536 | tf_op jit(solution)/shard_map/all_gather | solution.py:120
  232.5 20.7 %fusion = bf16[5120,640]{0,1:T(8,128)(2,1)} fusion(bf16[2048,5120]{1,0:T(8,128)(2,1)} %all-gather.2.cloned.1.call-done, bf16[2048,640]{1,0:T(8,128)(2,1)} %param.14, f32[2048]{0:T(1024)S(1)} %div.62), kind=kOutput, calls=%fused_computation.1 | convolution fusion | flops 13428981760 | bytes 30154752 | tf_op jit(solution)/shard_map/dot_general | solution.py:122
  253.2 9.5 %copy.104 = bf16[5120,640]{1,0:T(8,128)(2,1)} copy(bf16[5120,640]{0,1:T(8,128)(2,1)} %fusion) | data formatting | bytes 13107200
  262.7 0.0 copy-start.6
  262.7 0.0 reduce-scatter.4.cloned.1.call-update
  262.7 0.6 copy-done.6
  263.4 0.1 broadcast_in_dim.36
  263.4 0.1 lt.20
  263.5 0.0 copy-start.1
  263.5 9.7 %copy.78 = bf16[5120,640]{0,1:T(8,128)(2,1)} copy(bf16[5120,640]{1,0:T(8,128)(2,1)} %param.20) | data formatting | bytes 13107200 | tf_op args[7]
  273.3 0.0 copy-done.1
  273.3 1.8 fusion.32
  275.1 0.3 fusion.71
  275.4 0.1 maximum_bitcast_fusion
  275.5 0.3 multiply_cosine_fusion.1
  275.8 5.1 %fusion.12 = f32[4,32,5,128]{3,1,2,0:T(8,128)S(1)} fusion(bf16[5,128,5120,1]{2,1,0,3:T(8,128)(2,1)} %bitcast.105, bf16[4,32,5120]{2,1,0:T(8,128)(2,1)S(1)} %copy-done.1), kind=kOutput, calls=%fused_computation.11 | convolution fusion | flops 838860800 | bytes 8192000 | tf_op jit(solution)/shard_map/dot_general | solution.py:141
  280.9 0.2 subtract_convert_fusion.1
  281.1 0.1 pad_maximum_fusion
  281.2 0.1 iota_compare_fusion
  281.3 1.3 fusion.74
  282.6 0.0 copy-done
  282.6 0.0 copy-start.2
  282.7 0.8 fusion.73
  283.5 0.3 fusion.57
  283.8 0.5 fusion.49
  284.2 0.0 copy-done.2
  284.3 0.5 fusion.38
  284.8 0.7 copy-done.7
  285.4 0.6 fusion.26
  286.1 0.4 fusion.30
  286.5 0.2 copy.84
  286.7 0.2 broadcast_in_dim.68
  286.9 0.0 copy-start.3
  286.9 38.0 %all_to_all.38 = bf16[8,128,640]{1,2,0:T(8,128)(2,1)} all-to-all(bf16[8,128,640]{1,2,0:T(8,128)(2,1)S(1)} %broadcast_in_dim.68), channel_id=1, replica_groups=mesh['rep'=16,'tp'=8] {'tp'}, dimensions={0} | all-to-all | bytes 2621440 | tf_op jit(solution)/shard_map/all_to_all | solution.py:19
  324.9 6.1 %all-to-all-start.1 = ((bf16[128,16,320]{0,2,1:T(8,128)(2,1)}), bf16[128,16,320]{0,2,1:T(8,128)(2,1)}, u32[]{:S(2)}, u32[]{:S(2)}) async-start(bf16[128,16,320]{0,2,1:T(8,128)(2,1)} %bitcast.27), calls=%async_computation.1 | async-start | bytes 2621440 | tf_op jit(solution)/shard_map/all_to_all | solution.py:164
  331.0 0.0 copy-done.3
  331.0 1.3 copy.89
  332.3 2.5 copy.85
  334.9 0.0 copy-done.4
  334.9 1.3 copy.88
  336.1 33.8 %reduce-scatter.4.cloned.1.call-done = bf16[320,640]{1,0:T(8,128)(2,1)} async-done(((bf16[5120,640]{1,0:T(8,128)(2,1)}), bf16[320,640]{1,0:T(8,128)(2,1)}) %reduce-scatter.4.cloned.1.call-update) | async-done | bytes 409616
  370.0 2.0 copy.105
  371.9 2.3 fusion.44
  374.2 0.0 all-to-all-done.1
  374.2 3.4 fusion.14
  377.6 67.4 %all_to_all.39 = f32[16,128,640]{2,1,0:T(8,128)} all-to-all(f32[16,128,640]{2,1,0:T(8,128)S(1)} %fusion.14), channel_id=1, replica_groups=mesh['rep'=16,'tp'=8] {'rep'}, dimensions={0} | all-to-all | bytes 10485760 | tf_op jit(solution)/shard_map/all_to_all | solution.py:46
  445.0 2.7 reduce_sum.49
  447.8 1.2 broadcast_in_dim.71
  448.9 4.3 all-to-all-start.4
  453.2 1.2 copy.92
  454.4 18.6 %all-to-all-done.4 = bf16[8,128,640]{2,1,0:T(8,128)(2,1)} async-done(((bf16[8,128,640]{2,1,0:T(8,128)(2,1)}), bf16[8,128,640]{2,1,0:T(8,128)(2,1)}, u32[]{:S(2)}, u32[]{:S(2)}) %all-to-all-start.4) | async-done | bytes 1310752 | tf_op jit(solution)/shard_map/all_to_all | solution.py:19
  473.0 2.1 copy.91
  475.1 1.5 reshape_reshape.3
  (14 shorter events, 0.2 us)
Async XLA Ops:
  7.2 275.5 %copy-start = (bf16[32,256,128]{2,1,0:T(8,128)(2,1)S(1)}, bf16[32,256,128]{2,1,0:T(8,128)(2,1)}, u32[]{:S(2)}) copy-start(bf16[32,256,128]{2,1,0:T(8,128)(2,1)} %param.23) | copy-start | bytes 6291460
  7.2 0.8 copy-start.5
  7.2 225.3 %all-gather.2.cloned.1.call-start = ((), (), s32[]{:S(2)}) async-start(), calls=%async_computation.6 | async-start | bytes 23592960 | tf_op jit(solution)/shard_map/all_gather | solution.py:120
  7.9 362.0 %reduce-scatter.4.cloned.1.call-start = ((), (), s32[]{:S(2)}) async-start(), calls=%async_computation.7 | async-start | bytes 6963200
  262.7 0.7 copy-start.6
  263.5 9.8 %copy-start.1 = (bf16[4,32,5120]{2,1,0:T(8,128)(2,1)S(1)}, bf16[4,32,5120]{2,1,0:T(8,128)(2,1)}, u32[]{:S(2)}) copy-start(bf16[4,32,5120]{2,1,0:T(8,128)(2,1)} %param.19) | copy-start | bytes 3932164
  282.6 1.6 copy-start.2
  283.8 1.7 copy-start.7
  286.9 44.2 %copy-start.3 = (f32[320,640]{1,0:T(8,128)S(1)}, f32[320,640]{1,0:T(8,128)}, u32[]{:S(2)}) copy-start(f32[320,640]{1,0:T(8,128)} %param.16) | copy-start | bytes 2457604
  324.9 49.3 %all-to-all-start.1 = ((bf16[128,16,320]{0,2,1:T(8,128)(2,1)}), bf16[128,16,320]{0,2,1:T(8,128)(2,1)}, u32[]{:S(2)}, u32[]{:S(2)}) async-start(bf16[128,16,320]{0,2,1:T(8,128)(2,1)} %bitcast.27), calls=%async_computation.1 | async-start | bytes 2621440 | tf_op jit(solution)/shard_map/all_to_all | solution.py:164
  332.3 2.5 copy-start.4
  448.9 24.1 %all-to-all-start.4 = ((bf16[8,128,640]{2,1,0:T(8,128)(2,1)}), bf16[8,128,640]{2,1,0:T(8,128)(2,1)}, u32[]{:S(2)}, u32[]{:S(2)}) async-start(bf16[8,128,640]{2,1,0:T(8,128)(2,1)} %broadcast_in_dim.71), calls=%async_computation.4 | async-start | bytes 2621440 | tf_op jit(solution)/shard_map/all_to_all | solution.py:19
Sparse Core Ops, SparseCore 0:
  10.4 222.0 all-gather.1
  262.9 107.0 reduce-scatter.3
where the time goes:
time: 484 us; the launch traced here: 483 us
  waiting for transfers between devices  266 us (55%)
  blocking collectives  117 us (24%)
  matrix products  34.6 us (7%)
  local copies, waits for them, and re-layouts  34.5 us (7%)
  between operations  14.3 us (3%)
  starting transfers between devices  10.4 us (2%)
  other arithmetic  6.95 us (1%)
    all_gather x1, waiting for transfers between devices, per_device(): features = lax.all_gather(context, 'tp', axis=1, tiled=True)  213 us
    all_to_all x1, blocking collectives, sum_at_owner(): lax.all_to_all(tiles, axis, split_axis=0, concat_axis=0, tiled=True)  67.4 us
    all_to_all x2, blocking collectives, from_everyone(): lax.all_to_all(jnp.broadcast_to(array[None], (devices, *array.shape)), ax...  49.5 us
    unnamed x3, waiting for transfers between devices  34.5 us
    unnamed x24, local copies, waits for them, and re-layouts  28.9 us
    dot_general x1, matrix products, per_device(): lax.dot_general(features, scaled, (((0,), (0,)), ((), ())), preferred_ele...  20.7 us
    all_to_all x1, waiting for transfers between devices, from_everyone(): lax.all_to_all(jnp.broadcast_to(array[None], (devices, *array.shape)), ax...  18.6 us
  transfers between devices with their start and end apart: 4, of which 3 were waited for; matrix products, arithmetic and copies ran while one was open for 7% of the time, Pallas kernels for 0%

commit v1 on v0

--- a/solution.py
+++ b/solution.py
@@ -1,7 +1,351 @@
+import functools
 import jax
 import jax.numpy as jnp
 from jax import lax
+from jax.experimental import pallas as pl
+from jax.experimental.pallas import tpu as pltpu
 from jax.sharding import PartitionSpec as P
+
+MESH = pl.DeviceIdType.MESH
+LANE = 128
+CHUNKS = 5
+HALF = 1024
+
+
+def where_am_i():
+    rep = lax.axis_index("rep")
+    tp = lax.axis_index("tp")
+    return rep // 4, (rep // 2) % 2, rep % 2, tp // 2, tp % 2
+
+
+def device(x, yl, c, z, yh):
+    return {"rep": (x * 2 + yl) * 2 + c, "tp": z * 2 + yh}
+
+
+def gradient_kernel(
+    ctx, outg, rewards, counts, grad,
+    cb, sr, relay, ss, tot, totf, keep, give, got, part, xb, tb, ob,
+    load_sem, c_send, c_recv, f_send, f_recv, s_send, r_recv, r_send, p_recv,
+    t_send, t_recv, d_send, d_recv, x_send, x_recv, o_send, o_recv,
+):
+    x, yl, c, z, yh = where_am_i()
+    rep = lax.axis_index("rep")
+    tp = lax.axis_index("tp")
+    y = yh * 2 + yl
+    yp, ym = (y + 1) % 4, (y + 3) % 4
+    z_up = device(x, yl, c, (z + 1) % 4, yh)
+    z_dn = device(x, yl, c, (z + 3) % 4, yh)
+    y_up = device(x, yp % 2, c, z, yp // 2)
+    y_dn = device(x, ym % 2, c, z, ym // 2)
+    mate = device(x, yl, 1 - c, z, yh)
+
+    def load(src, dst, j, k):
+        return pltpu.make_async_copy(src.at[:, pl.ds(j * LANE, LANE)], dst, load_sem.at[k, j])
+
+    for j in range(CHUNKS):
+        load(ctx, cb.at[0, j], j, 0).start()
+        load(outg, sr.at[0, j], j, 1).start()
+
+    barrier = pltpu.get_barrier_semaphore()
+
+    def greet(target):
+        pl.semaphore_signal(barrier, inc=1, device_id=target, device_id_type=MESH)
+
+    @pl.loop(1, 16)
+    def _(d):
+        greet({"rep": (rep + d) % 16, "tp": tp})
+
+    for k in range(4):
+        greet(device(x, k // 2, k % 2, z, 1 - yh))
+    greet(z_up)
+    greet(z_dn)
+    pl.semaphore_wait(barrier, 21)
+
+    def send(src, dst, ss_, rs_, target):
+        return pltpu.make_async_remote_copy(
+            src_ref=src, dst_ref=dst, send_sem=ss_, recv_sem=rs_,
+            device_id=target, device_id_type=MESH,
+        )
+
+    tot[0] = counts[...]
+
+    def count_copy(d):
+        return send(counts, tot.at[d], t_send.at[d], t_recv.at[d], {"rep": (rep + d) % 16, "tp": tp})
+
+    @pl.loop(1, 16)
+    def _(d):
+        count_copy(d).start()
+
+    def own_up(j):
+        return send(cb.at[0, j], cb.at[1, j], c_send.at[0, j], c_recv.at[0, j], z_up)
+
+    def own_dn(j):
+        return send(cb.at[0, j], cb.at[3, j], c_send.at[1, j], c_recv.at[1, j], z_dn)
+
+    first, second = pl.ds(0, HALF), pl.ds(HALF, HALF)
+
+    def fwd_up(j):
+        return send(cb.at[1, j, first], cb.at[2, j, first], f_send.at[0, j], f_recv.at[0, j], z_up)
+
+    def fwd_dn(j):
+        return send(cb.at[3, j, second], cb.at[2, j, second], f_send.at[1, j], f_recv.at[1, j], z_dn)
+
+    def out_up(j):
+        return send(sr.at[0, j, first], relay.at[0, j], s_send.at[0, j], r_recv.at[0, j], y_up)
+
+    def out_dn(j):
+        return send(sr.at[0, j, second], relay.at[1, j], s_send.at[1, j], r_recv.at[1, j], y_dn)
+
+    def pass_up(j):
+        return send(relay.at[0, j], sr.at[1, j, first], r_send.at[0, j], p_recv.at[0, j], y_up)
+
+    def pass_dn(j):
+        return send(relay.at[1, j], sr.at[1, j, second], r_send.at[1, j], p_recv.at[1, j], y_dn)
+
+    def issue(j):
+        own_up(j).start()
+        own_dn(j).start()
+        out_up(j).start()
+        out_dn(j).start()
+
+    for j in range(CHUNKS):
+        load(ctx, cb.at[0, j], j, 0).wait()
+        load(outg, sr.at[0, j], j, 1).wait()
+        if j < 2:
+            issue(j)
+
+    @pl.loop(1, 16)
+    def _(d):
+        count_copy(d).wait()
+
+    totf[...] = jnp.sum(tot[...], axis=0) * (1.0 / 64.0)
+
+    def scale(rel):
+        @pl.loop(0, 32)
+        def _(seg):
+            rows = pl.ds(pl.multiple_of(seg * 64, 64), 64)
+            p = seg // 4
+            factor = (rewards[p, seg % 4].astype(jnp.float32) - totf[pl.ds(p, 1), :]) * (1.0 / 32768.0)
+            for j in range(CHUNKS):
+                ss[rel, rows, j * LANE : (j + 1) * LANE] = (
+                    sr[rel, j, rows, :].astype(jnp.float32) * factor
+                ).astype(jnp.bfloat16)
+
+    scale(0)
+
+    def step(j):
+        own_up(j).wait_recv()
+        fwd_up(j).start()
+        own_dn(j).wait_recv()
+        fwd_dn(j).start()
+        out_up(j).wait_recv()
+        pass_up(j).start()
+        out_dn(j).wait_recv()
+        pass_dn(j).start()
+        if j + 2 < CHUNKS:
+            issue(j + 2)
+
+    def far(j):
+        fwd_up(j).wait_recv()
+        fwd_dn(j).wait_recv()
+
+    def keeps(rel):
+        s = yh if rel == 0 else 1 - yh
+        return c == s
+
+    def hand(j, r):
+        return send(give.at[j, r], got.at[j, r], d_send.at[j, r], d_recv.at[j, r], mate)
+
+    def compute(j, rel):
+        mine = keeps(rel)
+
+        @pl.loop(0, 4)
+        def _(r):
+            block = lax.dot_general(
+                cb[r, j], ss[rel], (((0,), (0,)), ((), ())), preferred_element_type=jnp.float32
+            )
+
+            @pl.when(mine)
+            def _():
+                keep[j, r] = block
+
+            @pl.when(jnp.logical_not(mine))
+            def _():
+                give[j, r] = block.astype(jnp.bfloat16)
+                hand(j, r).start()
+
+    def over_x(j, dx):
+        to = (x + dx) % 4
+        r = (z - to + 4) % 4
+        return send(part.at[j, r], xb.at[j, dx - 1], x_send.at[j, dx - 1], x_recv.at[j, dx - 1],
+                    device(to, yl, c, z, yh))
+
+    def pair_sum(j, rel):
+        @pl.when(keeps(rel))
+        def _():
+            @pl.loop(0, 4)
+            def _(r):
+                hand(j, r).wait_recv()
+                part[j, r] = (keep[j, r] + got[j, r].astype(jnp.float32)).astype(jnp.bfloat16)
+
+            for dx in (2, 1, 3):
+                over_x(j, dx).start()
+
+    def pieces(j):
+        if j < 2:
+            return ((0, 128, 0, 128 * j, j),)
+        if j > 2:
+            return ((0, 128, 1, 128 * j - 320, j - 2),)
+        return ((0, 64, 0, 256, 2), (64, 64, 1, 0, 0))
+
+    def to_owner(j, piece, local):
+        at, rows, core, row, k = piece
+        src = tb.at[j, pl.ds(at, rows)]
+        dst = ob.at[yl, pl.ds(row, rows)]
+        if local:
+            return pltpu.make_async_copy(src, dst, o_recv.at[yl, k])
+        return send(src, dst, o_send.at[j, at // 64], o_recv.at[yl, k], device(x, yh, core, z, c))
+
+    def is_me(core):
+        return jnp.logical_and(jnp.logical_and(c == yh, yh == yl), c == core)
+
+    def x_sum(j, rel):
+        @pl.when(keeps(rel))
+        def _():
+            total = part[j, (z - x + 4) % 4].astype(jnp.float32)
+            for dx in (1, 2, 3):
+                over_x(j, dx).wait_recv()
+                total = total + xb[j, dx - 1].astype(jnp.float32)
+            tb[j] = total.astype(jnp.bfloat16)
+            for piece in pieces(j):
+                @pl.when(is_me(piece[2]))
+                def _():
+                    to_owner(j, piece, True).start()
+
+                @pl.when(jnp.logical_not(is_me(piece[2])))
+                def _():
+                    to_owner(j, piece, False).start()
+
+    step(0)
+    step(1)
+    far(0)
+    compute(0, 0)
+    step(2)
+    pair_sum(0, 0)
+    far(1)
+    compute(1, 0)
+    pair_sum(1, 0)
+    step(3)
+    x_sum(0, 0)
+    step(4)
+    for j in range(CHUNKS):
+        pass_up(j).wait_recv()
+        pass_dn(j).wait_recv()
+    scale(1)
+    compute(0, 1)
+    compute(1, 1)
+    pair_sum(0, 1)
+    far(2)
+    compute(2, 0)
+    pair_sum(1, 1)
+    x_sum(1, 0)
+    compute(2, 1)
+    pair_sum(2, 0)
+    x_sum(0, 1)
+    pair_sum(2, 1)
+    far(3)
+    compute(3, 0)
+    x_sum(1, 1)
+    compute(3, 1)
+    pair_sum(3, 0)
+    x_sum(2, 0)
+    pair_sum(3, 1)
+    x_sum(2, 1)
+    far(4)
+    compute(4, 0)
+    compute(4, 1)
+    pair_sum(4, 0)
+    pair_sum(4, 1)
+    x_sum(3, 0)
+    x_sum(3, 1)
+    x_sum(4, 0)
+    x_sum(4, 1)
+
+    sizes0 = (128, 128, 64)
+    rows0 = (0, 128, 256)
+    sizes1 = (64, 128, 128)
+    rows1 = (0, 64, 192)
+    for core, sizes, starts in ((0, sizes0, rows0), (1, sizes1, rows1)):
+        @pl.when(c == core)
+        def _():
+            for src in range(2):
+                for k in range(3):
+                    there = ob.at[src, pl.ds(starts[k], sizes[k])]
+                    pltpu.make_async_copy(there, there, o_recv.at[src, k]).wait()
+
+    grad[...] = ob[0].astype(jnp.float32) + ob[1].astype(jnp.float32)
+
+    for j in range(CHUNKS):
+        for copy in (own_up(j), own_dn(j), fwd_up(j), fwd_dn(j), out_up(j), out_dn(j), pass_up(j), pass_dn(j)):
+            copy.wait_send()
+
+        @pl.loop(0, 4)
+        def _(r):
+            hand(j, r).wait_send()
+
+        for dx in (1, 2, 3):
+            over_x(j, dx).wait_send()
+        for piece in pieces(j):
+            @pl.when(jnp.logical_not(is_me(piece[2])))
+            def _():
+                to_owner(j, piece, False).wait_send()
+
+
+def gradient_of(context, out_grad, rewards, counts):
+    bf, f32 = jnp.bfloat16, jnp.float32
+    dma = pltpu.SemaphoreType.DMA
+    tokens, width = context.shape
+    return pl.pallas_call(
+        gradient_kernel,
+        out_shape=jax.ShapeDtypeStruct((320, width), f32),
+        in_specs=[
+            pl.BlockSpec(memory_space=pl.ANY),
+            pl.BlockSpec(memory_space=pl.ANY),
+            pl.BlockSpec(memory_space=pltpu.SMEM),
+            pl.BlockSpec(memory_space=pltpu.VMEM),
+        ],
+        out_specs=pl.BlockSpec(memory_space=pltpu.VMEM),
+        scratch_shapes=[
+            pltpu.VMEM((4, CHUNKS, tokens, LANE), bf),
+            pltpu.VMEM((2, CHUNKS, tokens, LANE), bf),
+            pltpu.VMEM((2, CHUNKS, HALF, LANE), bf),
+            pltpu.VMEM((2, tokens, width), bf),
+            pltpu.VMEM((16, 8, LANE), f32),
+            pltpu.VMEM((8, LANE), f32),
+            pltpu.VMEM((CHUNKS, 4, LANE, width), f32),
+            pltpu.VMEM((CHUNKS, 4, LANE, width), bf),
+            pltpu.VMEM((CHUNKS, 4, LANE, width), bf),
+            pltpu.VMEM((CHUNKS, 4, LANE, width), bf),
+            pltpu.VMEM((CHUNKS, 3, LANE, width), bf),
+            pltpu.VMEM((CHUNKS, LANE, width), bf),
+            pltpu.VMEM((2, 320, width), bf),
+            dma((2, CHUNKS)),
+            dma((2, CHUNKS)), dma((2, CHUNKS)),
+            dma((2, CHUNKS)), dma((2, CHUNKS)),
+            dma((2, CHUNKS)), dma((2, CHUNKS)),
+            dma((2, CHUNKS)), dma((2, CHUNKS)),
+            dma((16,)), dma((16,)),
+            dma((CHUNKS, 4)), dma((CHUNKS, 4)),
+            dma((CHUNKS, 3)), dma((CHUNKS, 3)),
+            dma((CHUNKS, 2)), dma((2, 3)),
+        ],
+        compiler_params=pltpu.CompilerParams(
+            collective_id=0, has_side_effects=True, vmem_limit_bytes=60 * 1024 * 1024
+        ),
+        cost_estimate=pl.CostEstimate(flops=13_400_000_000, bytes_accessed=6_000_000, transcendentals=0),
+        name="gradient",
+    )(context, out_grad, rewards, counts)
+
 
 HEAD_DIM = 128
 
@@ -107,25 +451,10 @@
     cache_values,
     lengths,
 ):
-    replicas = lax.axis_size("rep")
-    prompt_count, local_group = rewards.shape
-    totals = of_everyone(jnp.sum(rewards, axis=1), "rep")
-    group_size = local_group * replicas
-    advantage = rewards.astype(jnp.float32) - totals.astype(jnp.float32)[:, None] / group_size
-    token_local = context.shape[0]
-    per_token = jnp.repeat(advantage.reshape(-1), token_local // (prompt_count * local_group)) / (
-        token_local * replicas
-    )
-    scaled = (out_grad.astype(jnp.float32) * per_token[:, None]).astype(jnp.bfloat16)
-    features = lax.all_gather(context, "tp", axis=1, tiled=True)
-    gradient = lax.psum_scatter(
-        lax.dot_general(
-            features, scaled, (((0,), (0,)), ((), ())), preferred_element_type=jnp.float32
-        ).astype(jnp.bfloat16),
-        "rep",
-        scatter_dimension=0,
-        tiled=True,
-    ).astype(jnp.float32)
+    counts = jnp.broadcast_to(
+        jnp.sum(rewards, axis=1).astype(jnp.float32)[:, None], (rewards.shape[0], LANE)
+    )
+    gradient = gradient_of(context, out_grad, rewards, counts)
     moment_new = first_beta * first_moment + (1.0 - first_beta) * gradient
     square_new = second_beta * second_moment + (1.0 - second_beta) * gradient * gradient
     adam_step = (

time: 484 us -> 297 us (0.61)
  waiting for transfers between devices: 266 us -> 19.4 us
  Pallas kernels: 0 us -> 127 us
  blocking collectives: 117 us -> 96.3 us
  matrix products: 34.6 us -> 14.6 us
  local copies, waits for them, and re-layouts: 34.5 us -> 16.8 us
  between operations: 14.3 us -> 0.84 us
    all_gather x1 -> x0, waiting for transfers between devices: 213 us -> none  [per_device(): features = lax.all_gather(context, 'tp', axis=1, tiled=True)]
    pallas_call x0 -> x1, Pallas kernels: none -> 127 us  [gradient_of(): pl.pallas_call(gradient_kernel, out_shape=jax.ShapeDtypeStruct((320, widt...]
    unnamed x3 -> x0, waiting for transfers between devices: 34.5 us -> none
    all_to_all x2 -> x1, blocking collectives: 49.5 us -> 22.9 us  [from_everyone(): lax.all_to_all(jnp.broadcast_to(array[None], (devices, *array.shape)), ax...]
    dot_general x1 -> x0, matrix products: 20.7 us -> none  [per_device(): lax.dot_general(features, scaled, (((0,), (0,)), ((), ())), preferred_ele...]
    unnamed x24 -> x21, local copies, waits for them, and re-layouts: 28.9 us -> 11.5 us
    all_to_all x1, blocking collectives: 67.4 us -> 73.4 us  [sum_at_owner(): lax.all_to_all(tiles, axis, split_axis=0, concat_axis=0, tiled=True)]
  transfers between devices with their start and end apart: 4 -> 2, of which waited for: 3 -> 1; matrix products, arithmetic and copies ran while one was open for 7% -> 1% of each run, Pallas kernels for 0% -> 43%
where the time goes in v1:
time: 297 us; the launch traced here: 296 us
  Pallas kernels  127 us (43%)
  blocking collectives  96.3 us (32%)
  waiting for transfers between devices  19.4 us (7%)
  local copies, waits for them, and re-layouts  16.8 us (6%)
  matrix products  14.6 us (5%)
  starting transfers between devices  12.7 us (4%)
  other arithmetic  8.3 us (3%)
    pallas_call x1, Pallas kernels, gradient_of(): pl.pallas_call(gradient_kernel, out_shape=jax.ShapeDtypeStruct((320, widt...  127 us
    all_to_all x1, blocking collectives, sum_at_owner(): lax.all_to_all(tiles, axis, split_axis=0, concat_axis=0, tiled=True)  73.4 us
    all_to_all x1, blocking collectives, from_everyone(): lax.all_to_all(jnp.broadcast_to(array[None], (devices, *array.shape)), ax...  22.9 us
    all_to_all x1, waiting for transfers between devices, from_everyone(): lax.all_to_all(jnp.broadcast_to(array[None], (devices, *array.shape)), ax...  19.3 us
    unnamed x21, local copies, waits for them, and re-layouts  11.5 us
    all_to_all x1, starting transfers between devices, from_everyone(): lax.all_to_all(jnp.broadcast_to(array[None], (devices, *array.shape)), ax...  8.19 us
  transfers between devices with their start and end apart: 2, of which 1 were waited for; matrix products, arithmetic and copies ran while one was open for 1% of the time, Pallas kernels for 43%

profile of v1, /device:TPU:0, one launch (start us, length us, event | category | flops | bytes accessed | tf_op | source)
XLA Modules:
  0.0 296.1 jit_solution(6554733246531298279)
XLA Ops:
  0.6 0.0 copy-start
  0.7 0.9 broadcast_in_dim.34
  1.5 0.1 lt.20
  1.6 0.1 iota_compare_fusion
  1.7 0.0 copy-start.1
  1.7 0.0 copy-start.3
  1.7 3.0 fusion.36
  4.7 0.0 copy-done.1
  4.7 0.0 copy-done.3
  4.7 0.5 fusion.30
  5.2 0.3 multiply_cosine_fusion.1
  5.5 0.9 fusion.67
  6.4 9.5 %copy.35 = bf16[5120,640]{0,1:T(8,128)(2,1)} copy(bf16[5120,640]{1,0:T(8,128)(2,1)} %param.20) | data formatting | bytes 13107200 | tf_op args[7]
  16.0 0.0 copy-start.4
  16.0 0.0 copy-start.5
  16.0 5.0 %fusion.10 = f32[4,32,5,128]{3,1,2,0:T(8,128)S(1)} fusion(bf16[5,128,5120,1]{2,1,0,3:T(8,128)(2,1)} %bitcast.101, bf16[4,32,5120]{2,1,0:T(8,128)(2,1)S(1)} %copy-done.1), kind=kOutput, calls=%fused_computation.6 | convolution fusion | flops 838860800 | bytes 8192000 | tf_op jit(solution)/shard_map/dot_general | solution.py:470
  21.0 0.0 copy-done.4
  21.0 0.0 copy-done.5
  21.0 0.1 maximum_bitcast_fusion
  21.1 0.2 subtract_convert_fusion.1
  21.3 0.1 pad_maximum_fusion
  21.4 1.3 fusion.70
  22.7 0.0 copy-done
  22.7 0.0 copy-start.8
  22.7 0.8 fusion.69
  23.6 0.3 fusion.53
  23.8 0.5 fusion.40
  24.3 0.0 copy-done.8
  24.3 0.0 copy-start.6
  24.3 0.6 fusion.24
  24.9 0.1 copy-done.6
  25.1 0.4 fusion.28
  25.5 0.2 copy.41
  25.7 1.2 broadcast_in_dim.63
  26.9 0.0 copy-start.7
  26.9 8.2 %all-to-all-start = ((bf16[8,128,640]{1,2,0:T(8,128)(2,1)}), bf16[8,128,640]{1,2,0:T(8,128)(2,1)S(1)}, u32[]{:S(2)}, u32[]{:S(2)}) async-start(bf16[8,128,640]{1,2,0:T(8,128)(2,1)} %broadcast_in_dim.63), calls=%async_computation | async-start | bytes 2621440 | tf_op jit(solution)/shard_map/all_to_all | solution.py:363
  35.1 0.0 copy-done.7
  35.1 0.7 copy.42.rewards
  35.8 19.3 %all-to-all-done = bf16[8,128,640]{1,2,0:T(8,128)(2,1)S(1)} async-done(((bf16[8,128,640]{1,2,0:T(8,128)(2,1)}), bf16[8,128,640]{1,2,0:T(8,128)(2,1)S(1)}, u32[]{:S(2)}, u32[]{:S(2)}) %all-to-all-start) | async-done | bytes 1310752 | tf_op jit(solution)/shard_map/all_to_all | solution.py:363
  55.2 0.0 copy-start.2
  55.2 1.1 copy-done.2
  56.2 4.5 %all-to-all-start.1 = ((bf16[128,16,320]{0,2,1:T(8,128)(2,1)}), bf16[128,16,320]{0,2,1:T(8,128)(2,1)S(1)}, u32[]{:S(2)}, u32[]{:S(2)}) async-start(bf16[128,16,320]{0,2,1:T(8,128)(2,1)} %bitcast.102), calls=%async_computation.1 | async-start | bytes 2621440 | tf_op jit(solution)/shard_map/all_to_all | solution.py:493
  60.7 0.7 broadcast_in_dim.64.counts
  61.4 127.1 %gradient.1 = f32[320,640]{1,0:T(8,128)} custom-call(bf16[2048,640]{1,0:T(8,128)(2,1)} %ctx.1, bf16[2048,640]{1,0:T(8,128)(2,1)} %outg.1, s32[8,4]{1,0:T(8,128)} %copy.42.rewards, f32[8,128]{1,0:T(8,128)} %broadcast_in_dim.64.counts), custom_call_target="tpu_custom_call" | custom-call | flops 13400000512 | bytes 6000000 | tf_op jit(solution)/shard_map/gradient/pallas_call | solution.py:308
  188.5 3.0 %fusion.45 = f32[320,640]{1,0:T(8,128)} fusion(f32[320,640]{1,0:T(8,128)} %gradient.1, f32[320,640]{1,0:T(8,128)} %param.18, f32[320,640]{1,0:T(8,128)} %param.17), kind=kLoop, calls=%fused_computation.34 | loop fusion | flops 2252800 | bytes 3276800 | tf_op jit(solution)/shard_map/div | solution.py:461
  191.6 0.0 all-to-all-done.1
  191.6 3.1 %fusion.12 = f32[16,128,640]{2,1,0:T(8,128)S(1)} fusion(bf16[128,16,320]{0,2,1:T(8,128)(2,1)S(1)} %all-to-all-done.1, f32[320,640]{1,0:T(8,128)} %param.16, f32[320,640]{1,0:T(8,128)} %fusion.45), kind=kOutput, calls=%fused_computation.8 | convolution fusion | flops 839475200 | bytes 8192000 | tf_op jit(solution)/shard_map/dot_general | solution.py:495
  194.7 73.4 %all_to_all.31 = f32[16,128,640]{2,1,0:T(8,128)} all-to-all(f32[16,128,640]{2,1,0:T(8,128)S(1)} %fusion.12), channel_id=1, replica_groups=mesh['rep'=16,'tp'=8] {'rep'}, dimensions={0} | all-to-all | bytes 10485760 | tf_op jit(solution)/shard_map/all_to_all | solution.py:390
  268.1 2.7 reduce_sum.39
  270.8 0.1 broadcast_in_dim.65
  270.9 22.9 %all_to_all.32 = bf16[8,128,640]{2,1,0:T(8,128)(2,1)S(1)} all-to-all(bf16[8,128,640]{2,1,0:T(8,128)(2,1)S(1)} %broadcast_in_dim.65), channel_id=1, replica_groups=mesh['rep'=16,'tp'=8] {'tp'}, dimensions={0} | all-to-all | bytes 2621440 | tf_op jit(solution)/shard_map/all_to_all | solution.py:363
  293.9 0.7 copy.43
  294.6 1.5 reshape_reshape.3
  (9 shorter events, 0.2 us)
Async XLA Ops:
  0.6 22.1 %copy-start = (bf16[32,256,128]{2,1,0:T(8,128)(2,1)S(1)}, bf16[32,256,128]{2,1,0:T(8,128)(2,1)}, u32[]{:S(2)}) copy-start(bf16[32,256,128]{2,1,0:T(8,128)(2,1)} %param.23) | copy-start | bytes 6291460
  1.7 3.0 %copy-start.1 = (bf16[4,32,5120]{2,1,0:T(8,128)(2,1)S(1)}, bf16[4,32,5120]{2,1,0:T(8,128)(2,1)}, u32[]{:S(2)}) copy-start(bf16[4,32,5120]{2,1,0:T(8,128)(2,1)} %param.19) | copy-start | bytes 3932164
  1.7 3.0 %copy-start.3 = (bf16[5120,128]{1,0:T(8,128)(2,1)S(1)}, bf16[5120,128]{1,0:T(8,128)(2,1)}, u32[]{:S(2)}) copy-start(bf16[5120,128]{1,0:T(8,128)(2,1)} %param.21) | copy-start | bytes 3932164
  16.0 5.0 %copy-start.4 = (bf16[4,32,64]{2,1,0:T(8,128)(2,1)S(1)}, bf16[4,32,64]{2,1,0:T(8,128)(2,1)}, u32[]{:S(2)}) copy-start(bf16[4,32,64]{2,1,0:T(8,128)(2,1)} %get-tuple-element.4) | copy-start | bytes 49156
  16.0 5.0 %copy-start.5 = (bf16[4,32,64]{2,1,0:T(8,128)(2,1)S(1)}, bf16[4,32,64]{2,1,0:T(8,128)(2,1)}, u32[]{:S(2)}) copy-start(bf16[4,32,64]{2,1,0:T(8,128)(2,1)} %get-tuple-element.5) | copy-start | bytes 49156
  22.7 1.6 copy-start.8
  24.3 0.8 copy-start.6
  26.9 8.2 %copy-start.7 = (s32[8,4]{0,1:T(4,128)S(1)}, s32[8,4]{0,1:T(4,128)}, u32[]{:S(2)}) copy-start(s32[8,4]{0,1:T(4,128)} %param.15) | copy-start | bytes 388
  26.9 28.2 %all-to-all-start = ((bf16[8,128,640]{1,2,0:T(8,128)(2,1)}), bf16[8,128,640]{1,2,0:T(8,128)(2,1)S(1)}, u32[]{:S(2)}, u32[]{:S(2)}) async-start(bf16[8,128,640]{1,2,0:T(8,128)(2,1)} %broadcast_in_dim.63), calls=%async_computation | async-start | bytes 2621440 | tf_op jit(solution)/shard_map/all_to_all | solution.py:363
  55.2 1.1 copy-start.2
  56.2 135.3 %all-to-all-start.1 = ((bf16[128,16,320]{0,2,1:T(8,128)(2,1)}), bf16[128,16,320]{0,2,1:T(8,128)(2,1)S(1)}, u32[]{:S(2)}, u32[]{:S(2)}) async-start(bf16[128,16,320]{0,2,1:T(8,128)(2,1)} %bitcast.102), calls=%async_computation.1 | async-start | bytes 2621440 | tf_op jit(solution)/shard_map/all_to_all | solution.py:493

commit v2 on v0

v2 whole, which is shorter than its diff:
```python
import jax
import jax.numpy as jnp
from jax import lax
from jax.experimental import pallas as pl
from jax.experimental.pallas import tpu as pltpu
from jax.sharding import PartitionSpec as P

HEAD_DIM = 128

rope_base = 1000000.0
first_beta = 0.9
second_beta = 0.95
adam_epsilon = 1e-08
step_count = 10
learn_rate = 0.001

MESH = pl.DeviceIdType.MESH
LANE = 128
CHUNKS = 5
HALF = 1024
SPANS = ((0, 3), (3, 2))
ROWS = 320
BF, F32 = jnp.bfloat16, jnp.float32


def device(x, yl, c, z, yh):
    return {"rep": (x * 2 + yl) * 2 + c, "tp": z * 2 + yh}


def step_kernel(
    ctx, outg, rewards, counts, heads, master, first_m, second_m,
    adam, decoded,
    cb, sr, ss, tot, totf, keep, give, got, part, xb, tb, ob,
    ag, hx, ab, aa, wb, dgive, dgot, dpart, dxb, dkeep, dys, dyb, dec,
    load_sem, c_send, c_recv, f_send, f_recv, s_send, s_recv,
    t_send, t_recv, d_send, d_recv, x_send, x_recv, o_send, o_recv,
    g_send, g_recv, i_send, i_recv, a_send, a_recv,
    e_send, e_recv, h_send, h_recv, y_send, y_recv, l_send, l_recv,
):
    rep = lax.axis_index("rep")
    tp = lax.axis_index("tp")
    x, yl, c, z, yh = rep // 4, (rep // 2) % 2, rep % 2, tp // 2, tp % 2
    z_up = device(x, yl, c, (z + 1) % 4, yh)
    z_dn = device(x, yl, c, (z + 3) % 4, yh)
    across = device(x, yl, c, z, 1 - yh)
    mate = device(x, yl, 1 - c, z, yh)
    beside = device(x, 1 - yl, c, z, yh)

    def load(src, dst, j, k):
        return pltpu.make_async_copy(src.at[:, pl.ds(j * LANE, LANE)], dst, load_sem.at[k, j])

    for j in range(CHUNKS):
        load(ctx, cb.at[0, j], j, 0).start()
        load(outg, sr.at[0, j], j, 1).start()

    barrier = pltpu.get_barrier_semaphore()

    def greet(target):
        pl.semaphore_signal(barrier, inc=1, device_id=target, device_id_type=MESH)

    @pl.loop(1, 32)
    def _(d):
        e = (rep * 2 + yh + d) % 32
        greet({"rep": e // 2, "tp": z * 2 + e % 2})

    @pl.loop(0, 6)
    def _(d):
        greet({"rep": rep, "tp": (z * 2 + 2 + d) % 8})

    pl.semaphore_wait(barrier, 37)

    def send(src, dst, ss_, rs_, target):
        return pltpu.make_async_remote_copy(
            src_ref=src, dst_ref=dst, send_sem=ss_, recv_sem=rs_,
            device_id=target, device_id_type=MESH,
        )

    first, second = pl.ds(0, HALF), pl.ds(HALF, HALF)

    def own_up(j):
        return send(cb.at[0, j], cb.at[1, j], c_send.at[0, j], c_recv.at[0, j], z_up)

    def own_dn(j):
        return send(cb.at[0, j], cb.at[3, j], c_send.at[1, j], c_recv.at[1, j], z_dn)

    def fwd_up(j):
        return send(cb.at[1, j, first], cb.at[2, j, first], f_send.at[0, j], f_recv.at[0, j], z_up)

    def fwd_dn(j):
        return send(cb.at[3, j, second], cb.at[2, j, second], f_send.at[1, j], f_recv.at[1, j], z_dn)

    def trade(j):
        return send(sr.at[0, j], sr.at[1, j], s_send.at[j], s_recv.at[j], across)

    def heads_z(dz):
        return send(heads, ag.at[dz], g_send.at[dz], g_recv.at[dz], device(x, yl, c, (z + dz) % 4, yh))

    @pl.loop(1, 4)
    def _(dz):
      heads_z(dz).start()

    for j in range(CHUNKS):
        load(ctx, cb.at[0, j], j, 0).wait()
        if j < 2:
            own_up(j).start()
            own_dn(j).start()
        load(outg, sr.at[0, j], j, 1).wait()
        if j < 2: trade(j).start()

    tot[0] = counts[...]

    def count_copy(d):
        return send(counts, tot.at[d], t_send.at[d], t_recv.at[d], {"rep": (rep + d) % 16, "tp": tp})

    @pl.loop(1, 16)
    def _(d):
        count_copy(d).start()

    @pl.loop(1, 16)
    def _(d):
        count_copy(d).wait()

    totf[...] = jnp.sum(tot[...], axis=0) * (1.0 / 64.0)

    def scale(rel):
        @pl.loop(0, 32)
        def _(seg):
            rows = pl.ds(pl.multiple_of(seg * 64, 64), 64)
            p = seg // 4
            factor = (rewards[p, seg % 4].astype(F32) - totf[pl.ds(p, 1), :]) * (1.0 / 32768.0)
            for j in range(CHUNKS):
                ss[rel, rows, j * LANE : (j + 1) * LANE] = (
                    sr[rel, j, rows, :].astype(F32) * factor
                ).astype(BF)

    scale(0)

    def step(j):
        own_up(j).wait_recv()
        fwd_up(j).start()
        own_dn(j).wait_recv()
        fwd_dn(j).start()
        if j + 2 < CHUNKS:
            own_up(j + 2).start()
            own_dn(j + 2).start()
        if j + 2 < CHUNKS:
            trade(j + 2).start()

    def far(j):
        fwd_up(j).wait_recv()
        fwd_dn(j).wait_recv()

    def hand(j, r):
        return send(give.at[j, r], got.at[j, r], d_send.at[j, r], d_recv.at[j, r], mate)

    def over_x(j, r, dx):
        slot = (dx + 3) % 4
        return send(part.at[j, r], xb.at[j, slot], x_send.at[j, slot], x_recv.at[j, slot],
                    device((x + dx) % 4, yl, c, z, yh))

    def contribute(low, high, rels):
        count = (high - low) * len(rels)

        def task(n):
            i = low + n // len(rels)
            rel = rels[0] + n % len(rels)
            rr = i % 4
            return i // 4, rr ^ (rr // 2), rel, (yh + rel) % 2 == c

        def compute(n):
            j, r, rel, mine = task(n)
            block = lax.dot_general(
                cb[r, j], ss[rel], (((0,), (0,)), ((), ())), preferred_element_type=F32
            )

            @pl.when(mine)
            def _():
                keep[n // len(rels)] = block

            @pl.when(jnp.logical_not(mine))
            def _():
                give[j, r] = block.astype(BF)
                hand(j, r).start()

        def pair(n):
            j, r, rel, mine = task(n)

            @pl.when(mine)
            def _():
                hand(j, r).wait_recv()
                part[j, r] = (keep[n // len(rels)] + got[j, r].astype(F32)).astype(BF)
                dx = (z - r - x + 8) % 4

                @pl.when(dx != 0)
                def _():
                    over_x(j, r, dx).start()

        @pl.loop(0, count + 2)
        def _(n):
            @pl.when(n < count)
            def _():
                compute(n)

            @pl.when(n >= 2)
            def _():
                pair(n - 2)

    def pieces(j):
        if j < 2:
            return ((0, 128, 0, 128 * j, j),)
        if j > 2:
            return ((0, 128, 1, 128 * j - ROWS, j - 2),)
        return ((0, 64, 0, 256, 2), (64, 64, 1, 0, 0))

    def to_owner(j, piece, local):
        at, rows, core, row, k = piece
        src = tb.at[j, pl.ds(at, rows)]
        dst = ob.at[yl, pl.ds(row, rows)]
        if local:
            return pltpu.make_async_copy(src, dst, o_recv.at[yl, k])
        return send(src, dst, o_send.at[j, at // 64], o_recv.at[yl, k], device(x, yh, core, z, c))

    def is_me(core):
        return jnp.logical_and(jnp.logical_and(c == yh, yh == yl), c == core)

    def x_sum(j):
        total = part[j, (z - x + 4) % 4].astype(F32)
        for slot in range(3):
            over_x(j, 0, slot + 1).wait_recv()
            total = total + xb[j, slot].astype(F32)
        tb[j] = total.astype(BF)
        for piece in pieces(j):
            @pl.when(is_me(piece[2]))
            def _():
                to_owner(j, piece, True).start()

            @pl.when(jnp.logical_not(is_me(piece[2])))
            def _():
                to_owner(j, piece, False).start()

    def heads_x(dz, local):
        to = (z - dz + 4) % 4
        if local:
            return pltpu.make_async_copy(ag.at[dz], hx.at[x], i_recv.at[x])
        return send(ag.at[dz], hx.at[x], i_send.at[dz], i_recv.at[x], device(to, yl, c, z, yh))

    def stays_x(dz):
        return (z - dz + 4) % 4 == x

    def heads_over_x():
        ag[0] = heads[...]
        for dz in (1, 2, 3):
            heads_z(dz).wait_recv()

        @pl.loop(0, 4)
        def _(dz):
            @pl.when(stays_x(dz))
            def _():
                heads_x(dz, True).start()

            @pl.when(jnp.logical_not(stays_x(dz)))
            def _():
                heads_x(dz, False).start()

    def spread(h, other, local):
        src = hx.at[:, pl.ds(h * ROWS, ROWS)]
        dst = ab.at[yl * 2 + c]
        if local:
            return pltpu.make_async_copy(src, dst, a_recv.at[yl * 2 + c])
        return send(src, dst, a_send.at[h, other], a_recv.at[yl * 2 + c], device(x, yh, h, z, other))

    def stays(h, other):
        return jnp.logical_and(yh == yl, jnp.logical_and(h == c, other == yh))

    def spread_heads():

        @pl.loop(0, 4)
        def _(k):
            pltpu.make_async_copy(hx.at[k], hx.at[k], i_recv.at[k]).wait()

        for h in range(2):
            for other in range(2):
                @pl.when(stays(h, other))
                def _():
                    spread(h, other, True).start()

                @pl.when(jnp.logical_not(stays(h, other)))
                def _():
                    spread(h, other, False).start()

    def take_heads():
        for k in range(4):
            pltpu.make_async_copy(ab.at[k], ab.at[k], a_recv.at[k]).wait()

        @pl.loop(0, 16)
        def _(g):
            aa[g] = ab[g // 4, g % 4].T

    step(0)
    contribute(0, 3, (0,))
    heads_over_x()
    step(1)
    contribute(4, 7, (0,))
    far(0)
    contribute(3, 4, (0,))
    step(2)
    contribute(8, 11, (0,))
    far(1)
    contribute(7, 8, (0,))
    step(3)
    contribute(12, 15, (0,))
    for j in range(CHUNKS):
        trade(j).wait_recv()
    spread_heads()
    scale(1)
    contribute(0, 11, (1,))
    far(2)
    contribute(11, 12, (0, 1))
    contribute(12, 15, (1,))
    step(4)
    contribute(16, 19, (0, 1))
    x_sum(0)
    x_sum(1)
    far(3)
    contribute(15, 16, (0, 1))
    x_sum(2)
    take_heads()
    far(4)
    contribute(19, 20, (0, 1))
    x_sum(3)
    x_sum(4)

    for core, sizes, starts in ((0, (128, 128, 64), (0, 128, 256)), (1, (64, 128, 128), (0, 64, 192))):
        @pl.when(c == core)
        def _():
            for src in range(2):
                for k in range(3):
                    there = ob.at[src, pl.ds(starts[k], sizes[k])]
                    pltpu.make_async_copy(there, there, o_recv.at[src, k]).wait()

    @pl.loop(0, ROWS // 32)
    def _(n):
        rows = pl.ds(pl.multiple_of(n * 32, 32), 32)
        gradient = ob[0, rows, :].astype(F32) + ob[1, rows, :].astype(F32)
        moment_new = first_beta * first_m[rows, :] + (1.0 - first_beta) * gradient
        square_new = second_beta * second_m[rows, :] + (1.0 - second_beta) * gradient * gradient
        direction = (
            moment_new
            / (1.0 - first_beta**step_count)
            / (jnp.sqrt(square_new / (1.0 - second_beta**step_count)) + adam_epsilon)
        )
        adam[rows, :] = direction
        wb[rows, :] = (master[rows, :] - learn_rate * direction).astype(BF)

    def blocks(q):
        return pl.ds(*SPANS[q])

    def d_hand(q, xg):
        return send(dgive.at[xg, :, blocks(q)], dgot.at[xg, :, blocks(q)], e_send.at[q, xg], e_recv.at[q, xg], mate)

    def d_over_x(q, dx):
        slot = (dx + 3) % 4
        to = (x + dx) % 4
        return send(dpart.at[to, :, blocks(q)], dxb.at[slot, :, blocks(q)], h_send.at[q, slot], h_recv.at[q, slot],
                    device(to, yl, c, z, yh))

    def d_beside(q):
        return send(dys.at[blocks(q)], dyb.at[blocks(q)], y_send.at[q], y_recv.at[q], beside)

    def d_across(q):
        there = dec.at[tp, blocks(q)]
        return send(there, there, l_send.at[q, 0], l_recv.at[q, tp], across)

    def d_over_z(q, dz, other):
        mine = z * 2 + (1 - yh if other else yh)
        there = dec.at[mine, blocks(q)]
        return send(there, there, l_send.at[q, dz + 3 * other], l_recv.at[q, mine],
                    device(x, yl, c, (z + dz) % 4, yh))

    def d_multiply(q):
        start, width = SPANS[q]
        columns = slice(start * LANE, (start + width) * LANE)

        @pl.loop(0, 8)
        def _(n):
            xg, side = (x + n // 2 + 2) % 4, n % 2
            block = jnp.dot(aa[side * 8 + (1 - c) * 4 + xg], wb[:, columns], preferred_element_type=F32)
            for b in range(width):
                dgive[xg, side, start + b] = block[:, b * LANE : (b + 1) * LANE].astype(BF)

            @pl.when(side == 1)
            def _():
                d_hand(q, xg).start()

        @pl.loop(0, 8)
        def _(n):
            dx, side = (n // 2 + 2) % 4, n % 2
            xg = (x + dx) % 4
            block = jnp.dot(aa[side * 8 + c * 4 + xg], wb[:, columns], preferred_element_type=F32)

            @pl.when(side == 0)
            def _():
                d_hand(q, xg).wait_recv()

            for b in range(width):
                dpart[xg, side, start + b] = (
                    block[:, b * LANE : (b + 1) * LANE] + dgot[xg, side, start + b].astype(F32)
                ).astype(BF)

            if q == 0:
                @pl.when(jnp.logical_and(side == 1, dx != 0))
                def _():
                    d_over_x(q, dx).start()

    def d_x_sum(q):
        start, width = SPANS[q]
        for dx in (1, 3, 2):
            d_over_x(q, dx).wait_recv()

        def total(side, b):
            value = dpart[x, side, b].astype(F32)
            for slot in range(3):
                value = value + dxb[slot, side, b].astype(F32)
            return value

        for b in range(start, start + width):
            dys[b] = total(1 - yl, b).astype(BF)
        d_beside(q).start()
        for b in range(start, start + width):
            dkeep[b] = total(yl, b)

    def d_finish(q):
        start, width = SPANS[q]
        d_beside(q).wait_recv()
        for b in range(start, start + width):
            dec[tp, b] = (dkeep[b] + dyb[b].astype(F32)).astype(BF)
        for dz in (2, 1, 3):
            d_over_z(q, dz, 0).start()
        d_across(q).start()

    def d_pass(q):
        other = dec.at[z * 2 + 1 - yh, blocks(q)]
        pltpu.make_async_copy(other, other, l_recv.at[q, z * 2 + 1 - yh]).wait()
        for dz in (2, 1, 3):
            d_over_z(q, dz, 1).start()

    d_multiply(0)
    if len(SPANS) > 1:
        d_multiply(1)
    d_x_sum(0)
    if len(SPANS) > 1:
        for dx in (2, 1, 3):
            d_over_x(1, dx).start()
    d_finish(0)
    d_pass(0)
    if len(SPANS) > 1:
        d_x_sum(1)
        d_finish(1)
        d_pass(1)

    for q in range(len(SPANS)):
        start, width = SPANS[q]

        @pl.loop(2, 8)
        def _(d):
            t = (z * 2 + d) % 8
            pltpu.make_async_copy(dec.at[t, blocks(q)], dec.at[t, blocks(q)], l_recv.at[q, t]).wait()

        for t in range(8):
            for b in range(start, start + width):
                decoded[:, t * 640 + b * LANE : t * 640 + (b + 1) * LANE] = dec[t, b]

    for j in range(CHUNKS):
        for copy in (own_up(j), own_dn(j), fwd_up(j), fwd_dn(j)) + (trade(j),):
            copy.wait_send()

        @pl.loop(0, 4)
        def _(r):
          hand(j, r).wait_send()

        if j < len(SPANS):
          @pl.loop(0, 4)
          def _(k):
            d_hand(j, k).wait_send()

          d_beside(j).wait_send()
          d_across(j).wait_send()
          for dz in (1, 2, 3):
            d_over_x(j, dz).wait_send()
            d_over_z(j, dz, 0).wait_send()
            d_over_z(j, dz, 1).wait_send()

        for dx in (1, 2, 3):
            over_x(j, 0, dx).wait_send()
        for piece in pieces(j):
          @pl.when(jnp.logical_not(is_me(piece[2])))
          def _():
              to_owner(j, piece, False).wait_send()

    for dz in (1, 2, 3):
      heads_z(dz).wait_send()

    @pl.loop(0, 4)
    def _(dz):
      @pl.when(jnp.logical_not(stays_x(dz)))
      def _():
          heads_x(dz, False).wait_send()

    for h in range(2):
      for other in range(2):
          @pl.when(jnp.logical_not(stays(h, other)))
          def _():
              spread(h, other, False).wait_send()


def learn_and_decode(context, out_grad, rewards, counts, heads, master, first_moment, second_moment):
    dma = pltpu.SemaphoreType.DMA
    vmem = pltpu.VMEM
    tokens, width = context.shape
    grid_all = [pl.BlockSpec(memory_space=pl.ANY)] * 2 + [pl.BlockSpec(memory_space=pltpu.SMEM)]
    grid_all += [pl.BlockSpec(memory_space=pltpu.VMEM)] * 5
    return pl.pallas_call(
        step_kernel,
        out_shape=(
            jax.ShapeDtypeStruct((ROWS, width), F32),
            jax.ShapeDtypeStruct((LANE, 8 * width), BF),
        ),
        in_specs=grid_all,
        out_specs=(pl.BlockSpec(memory_space=pltpu.VMEM), pl.BlockSpec(memory_space=pltpu.VMEM)),
        scratch_shapes=[
            vmem((4, CHUNKS, tokens, LANE), BF),
            vmem((2, CHUNKS, tokens, LANE), BF),
            vmem((2, tokens, width), BF),
            vmem((16, 8, LANE), F32),
            vmem((8, LANE), F32),
            vmem((12, LANE, width), F32),
            vmem((CHUNKS, 4, LANE, width), BF),
            vmem((CHUNKS, 4, LANE, width), BF),
            vmem((CHUNKS, 4, LANE, width), BF),
            vmem((CHUNKS, 3, LANE, width), BF),
            vmem((CHUNKS, LANE, width), BF),
            vmem((2, ROWS, width), BF),
            vmem((4, width, LANE), BF),
            vmem((4, width, LANE), BF),
            vmem((4, 4, ROWS, LANE), BF),
            vmem((16, LANE, ROWS), BF),
            vmem((ROWS, width), BF),
            vmem((4, 2, CHUNKS, LANE, LANE), BF),
            vmem((4, 2, CHUNKS, LANE, LANE), BF),
            vmem((4, 2, CHUNKS, LANE, LANE), BF),
            vmem((3, 2, CHUNKS, LANE, LANE), BF),
            vmem((CHUNKS, LANE, LANE), F32),
            vmem((CHUNKS, LANE, LANE), BF),
            vmem((CHUNKS, LANE, LANE), BF),
            vmem((8, CHUNKS, LANE, LANE), BF),
            dma((2, CHUNKS)),
            dma((2, CHUNKS)), dma((2, CHUNKS)),
            dma((2, CHUNKS)), dma((2, CHUNKS)),
            dma((CHUNKS,)), dma((CHUNKS,)),
            dma((16,)), dma((16,)),
            dma((CHUNKS, 4)), dma((CHUNKS, 4)),
            dma((CHUNKS, 3)), dma((CHUNKS, 3)),
            dma((CHUNKS, 2)), dma((2, 3)),
            dma((4,)), dma((4,)),
            dma((4,)), dma((4,)),
            dma((2, 2)), dma((4,)),
            dma((2, 4)), dma((2, 4)),
            dma((2, 3)), dma((2, 3)),
            dma((2,)), dma((2,)),
            dma((2, 7)), dma((2, 8)),
        ],
        compiler_params=pltpu.CompilerParams(
            collective_id=0, has_side_effects=True, vmem_limit_bytes=62 * 1024 * 1024
        ),
        cost_estimate=pl.CostEstimate(flops=14_300_000_000, bytes_accessed=10_000_000, transcendentals=0),
        name="learn_and_decode",
    )(context, out_grad, rewards, counts, heads, master, first_moment, second_moment)


def rotate(vectors, positions):
    half_dim = vectors.shape[-1] // 2
    frequency = rope_base ** (-2.0 * jnp.arange(half_dim, dtype=jnp.float32) / vectors.shape[-1])
    angles = positions[..., None].astype(jnp.float32) * frequency
    cosine_table = jnp.cos(angles)
    sine_table = jnp.sin(angles)
    former = vectors[..., :half_dim]
    latter = vectors[..., half_dim:]
    return jnp.concatenate(
        [former * cosine_table - latter * sine_table, latter * cosine_table + former * sine_table],
        axis=-1,
    )


def attend(queries, old_keys, old_values, new_keys, new_values, live_mask):
    score_scale = HEAD_DIM ** (-0.5)
    step_total = queries.shape[0]
    cache_scores = (
        jnp.einsum("tsgqd,scgd->tsgqc", queries, old_keys, preferred_element_type=jnp.float32)
        * score_scale
    )
    cache_scores = jnp.where(live_mask[None, :, None, None, :], cache_scores, -1e30)
    recent = (
        jnp.einsum("tsgqd,usgd->tsgqu", queries, new_keys, preferred_element_type=jnp.float32)
        * score_scale
    )
    causal = jnp.arange(step_total)[:, None] >= jnp.arange(step_total)[None, :]
    recent = jnp.where(causal[:, None, None, None, :], recent, -1e30)
    row_peak = jnp.maximum(jnp.max(cache_scores, axis=-1), jnp.max(recent, axis=-1))[..., None]
    cache_exp = jnp.exp(cache_scores - row_peak)
    recent_exp = jnp.exp(recent - row_peak)
    denominator = jnp.sum(cache_exp, axis=-1, keepdims=True) + jnp.sum(
        recent_exp, axis=-1, keepdims=True
    )
    cache_weight = (cache_exp / denominator).astype(jnp.bfloat16)
    recent_weight = (recent_exp / denominator).astype(jnp.bfloat16)
    attended = jnp.einsum(
        "tsgqc,scgd->tsgqd", cache_weight, old_values, preferred_element_type=jnp.float32
    )
    attended = attended + jnp.einsum(
        "tsgqu,usgd->tsgqd", recent_weight, new_values, preferred_element_type=jnp.float32
    )
    return attended.astype(jnp.bfloat16)


def per_device(
    context,
    out_grad,
    rewards,
    master,
    first_moment,
    second_moment,
    inputs,
    w_query,
    w_key,
    w_value,
    cache_keys,
    cache_values,
    lengths,
):
    counts = jnp.broadcast_to(
        jnp.sum(rewards, axis=1).astype(F32)[:, None], (rewards.shape[0], LANE)
    )
    step_total, seq_local, model_width = inputs.shape
    local_heads = w_query.shape[1] // HEAD_DIM
    local_kv = w_key.shape[1] // HEAD_DIM
    flat_rows = inputs.reshape(step_total * seq_local, model_width)
    projected = lax.optimization_barrier(jnp.dot(flat_rows, w_query, preferred_element_type=F32))
    queries = projected.reshape(step_total, seq_local, local_heads, HEAD_DIM)
    key_new = jnp.dot(flat_rows, w_key, preferred_element_type=F32).reshape(
        step_total, seq_local, local_kv, HEAD_DIM
    )
    value_new = (
        jnp.dot(flat_rows, w_value, preferred_element_type=F32)
        .reshape(step_total, seq_local, local_kv, HEAD_DIM)
        .astype(BF)
    )
    seq_length = jnp.repeat(lengths, seq_local // lengths.shape[0])
    positions = seq_length[None, :] + jnp.arange(step_total, dtype=jnp.int32)[:, None]
    queries = rotate(queries, positions[:, :, None]).astype(BF)
    queries = queries.reshape(step_total, seq_local, local_kv, local_heads // local_kv, HEAD_DIM)
    key_new = rotate(key_new, positions[:, :, None]).astype(BF)
    slot_total = cache_keys.shape[1]
    old_keys = cache_keys.reshape(seq_local, slot_total, local_kv, HEAD_DIM)
    old_values = cache_values.reshape(seq_local, slot_total, local_kv, HEAD_DIM)
    live_mask = jnp.arange(slot_total, dtype=jnp.int32)[None, :] < seq_length[:, None]
    attended = attend(queries, old_keys, old_values, key_new, value_new, live_mask)
    heads = attended.reshape(step_total * seq_local, local_heads * HEAD_DIM).T
    adam_step, decoded = learn_and_decode(
        context, out_grad, rewards, counts, heads, master, first_moment, second_moment
    )
    return (decoded.reshape(step_total, seq_local, model_width), adam_step)


def solution(mesh):
    placed = (
        P("rep", "tp"),
        P("rep", "tp"),
        P(None, "rep"),
        P("rep", "tp"),
        P("rep", "tp"),
        P("rep", "tp"),
        P(None, "rep", None),
        P(None, "tp"),
        P(None, "tp"),
        P(None, "tp"),
        P("rep", None, "tp"),
        P("rep", None, "tp"),
        P("rep"),
    )
    return jax.shard_map(
        per_device,
        mesh=mesh,
        in_specs=placed,
        out_specs=(P(None, "rep", None), P("rep", "tp")),
        check_vma=False,
    )
```

time: 484 us -> 194 us (0.40)
  waiting for transfers between devices: 266 us -> 0 us
  Pallas kernels: 0 us -> 171 us
  blocking collectives: 117 us -> 0 us
  local copies, waits for them, and re-layouts: 34.5 us -> 8.87 us
  matrix products: 34.6 us -> 9.63 us
  between operations: 14.3 us -> 0.79 us
  starting transfers between devices: 10.4 us -> 0 us
    all_gather x1 -> x0, waiting for transfers between devices: 213 us -> none  [per_device(): features = lax.all_gather(context, 'tp', axis=1, tiled=True)]
    pallas_call x0 -> x1, Pallas kernels: none -> 171 us  [learn_and_decode(): pl.pallas_call(step_kernel, out_shape=(jax.ShapeDtypeStruct((ROWS, width)...]
    all_to_all x3 -> x0, blocking collectives: 117 us -> none  [the longest x1 67.4 us: sum_at_owner(): lax.all_to_all(tiles, axis, split_axis=0, concat_axis=0, tiled=True)]
    unnamed x3 -> x0, waiting for transfers between devices: 34.5 us -> none
    dot_general x5 -> x3, matrix products: 31.5 us -> 6.46 us  [the longest x1 4.06 us: per_device(): jnp.dot(flat_rows, w_query, preferred_element_type=F32)]
    unnamed x24 -> x14, local copies, waits for them, and re-layouts: 28.9 us -> 6.2 us
    all_to_all x2 -> x0, waiting for transfers between devices: 18.6 us -> none  [the longest x1 18.6 us: from_everyone(): lax.all_to_all(jnp.broadcast_to(array[None], (devices, *array.shape)), ax...]
    all_to_all x2 -> x0, starting transfers between devices: 10.4 us -> none  [the longest x1 6.1 us: per_device(): lax.all_to_all(all_heads, 'rep', split_axis=1, concat_axis=0, tiled=True)]
  transfers between devices with their start and end apart: 4 -> 0, of which waited for: 3 -> 0; matrix products, arithmetic and copies ran while one was open for 7% -> 0% of each run, Pallas kernels for 0% -> 0%
where the time goes in v2:
time: 194 us; the launch traced here: 193 us
  Pallas kernels  171 us (88%)
  matrix products  9.63 us (5%)
  local copies, waits for them, and re-layouts  8.87 us (5%)
  other arithmetic  2.65 us (1%)
    pallas_call x1, Pallas kernels, learn_and_decode(): pl.pallas_call(step_kernel, out_shape=(jax.ShapeDtypeStruct((ROWS, width)...  171 us
    unnamed x14, local copies, waits for them, and re-layouts  6.2 us
    dot_general x1, matrix products, per_device(): jnp.dot(flat_rows, w_query, preferred_element_type=F32)  4.06 us

profile of v2, /device:TPU:0, one launch (start us, length us, event | category | flops | bytes accessed | tf_op | source)
XLA Modules:
  0.0 193.3 jit_solution(5150130813828186266)
XLA Ops:
  0.6 0.0 copy-start
  0.6 1.3 copy-done
  2.0 0.7 reduce_sum.27
  2.7 0.7 broadcast_in_dim.29
  3.4 0.1 lt.20
  3.5 0.7 broadcast_in_dim.24.counts
  4.2 1.3 copy.27.rewards
  5.5 0.1 iota_compare_fusion
  5.6 0.1 copy.22
  5.7 0.0 copy-start.2
  5.7 1.9 fusion.29
  7.6 0.0 copy-done.2
  7.6 0.5 fusion.26
  8.1 0.3 fusion.49
  8.4 0.1 maximum_bitcast_fusion
  8.5 0.5 multiply_cosine_fusion.1
  9.1 4.1 %fusion.55 = f32[128,640]{1,0:T(8,128)S(1)} fusion(bf16[128,5120]{1,0:T(8,128)(2,1)S(1)} %bitcast.86, bf16[5120,640]{1,0:T(8,128)(2,1)} %param.20), kind=kOutput, calls=%fused_computation.61 | convolution fusion | flops 838860800 | bytes 8192000 | tf_op jit(solution)/shard_map/dot_general | solution.py:647
  13.1 0.1 reshape.197
  13.2 0.2 fusion.52
  13.4 0.0 copy-start.1
  13.4 0.1 subtract_convert_fusion
  13.5 1.4 fusion.54
  14.9 0.1 copy-done.1
  15.0 0.0 copy-start.4
  15.0 0.8 fusion.53
  15.8 0.3 fusion.36
  16.1 0.5 fusion.33
  16.6 0.0 copy-done.4
  16.6 0.6 fusion.20
  17.2 0.4 fusion.24
  17.7 0.8 copy.26
  18.5 171.3 %learn_and_decode.1 = (f32[320,640]{1,0:T(8,128)}, bf16[128,5120]{1,0:T(8,128)(2,1)}) custom-call(bf16[2048,640]{1,0:T(8,128)(2,1)} %ctx.1, bf16[2048,640]{1,0:T(8,128)(2,1)} %outg.1, s32[8,4]{1,0:T(8,128)} %copy.27.rewards, f32[8,128]{1,0:T(8,128)} %broadcast_in_dim.24.counts, bf16[640,128]{1,0:T(8,128)(2,1)} %bitcast.90, f32[320,640]{1,0:T(8,128)} %master.1, ...), custom_call_target="tpu_custom_call" | custom-call | flops 14300000256 | bytes 10000000 | tf_op jit(solution)/shard_map/learn_and_decode/pallas_call | solution.py:522
  189.8 0.0 copy-start.3
  189.8 2.5 %copy.53 = bf16[4,32,5120]{2,1,0:T(8,128)(2,1)} copy(bf16[4,32,5120]{2,1,0:T(8,128)(2,1)} %bitcast.87) | data formatting | bytes 2621440
  192.4 0.0 copy-done.3
  192.4 0.9 copy.54
  (8 shorter events, 0.1 us)
Async XLA Ops:
  0.6 1.3 copy-start
  5.7 1.9 copy-start.2
  13.4 1.6 copy-start.1
  15.0 1.6 copy-start.4
  189.8 2.5 %copy-start.3 = (f32[320,640]{1,0:T(8,128)S(1)}, f32[320,640]{1,0:T(8,128)}, u32[]{:S(2)}) copy-start(f32[320,640]{1,0:T(8,128)} %get-tuple-element.21) | copy-start | bytes 2457604

commit v3 on v2

--- a/solution.py
+++ b/solution.py
@@ -20,6 +20,7 @@
 HALF = 1024
 SPANS = ((0, 3), (3, 2))
 ROWS = 320
+CACHE = 256
 BF, F32 = jnp.bfloat16, jnp.float32
 
 
@@ -28,7 +29,8 @@
 
 
 def step_kernel(
-    ctx, outg, rewards, counts, heads, master, first_m, second_m,
+    ctx, outg, rewards, lengths, cosine, sine, tokens_in, w_query, w_query_rows, w_key, w_value,
+    old_keys, old_values, master_in, first_in, second_in,
     adam, decoded,
     cb, sr, ss, tot, totf, keep, give, got, part, xb, tb, ob,
     ag, hx, ab, aa, wb, dgive, dgot, dpart, dxb, dkeep, dys, dyb, dec,
@@ -36,6 +38,8 @@
     t_send, t_recv, d_send, d_recv, x_send, x_recv, o_send, o_recv,
     g_send, g_recv, i_send, i_recv, a_send, a_recv,
     e_send, e_recv, h_send, h_recv, y_send, y_recv, l_send, l_recv,
+    xs, qa, ka, va, qb, kn, vn, kf, vf, att, hb, master, first_m, second_m,
+    w_sem, k_sem, m_sem,
 ):
     rep = lax.axis_index("rep")
     tp = lax.axis_index("tp")
@@ -53,6 +57,34 @@
         load(ctx, cb.at[0, j], j, 0).start()
         load(outg, sr.at[0, j], j, 1).start()
 
+    weight_loads = (
+        pltpu.make_async_copy(w_query.at[pl.ds(0, 3)], give.at[pl.ds(2, 3)], w_sem.at[0]),
+        pltpu.make_async_copy(w_query.at[pl.ds(3, 3)], part.at[pl.ds(2, 3)], w_sem.at[1]),
+        pltpu.make_async_copy(w_query_rows.at[pl.ds(3072, 2048)], ss.at[1], w_sem.at[4]),
+        pltpu.make_async_copy(w_key, dgive, w_sem.at[2]),
+        pltpu.make_async_copy(w_value, dpart, w_sem.at[3]),
+    )
+
+    def cache_loads(g):
+        seqs = pl.ds(g * 8, 8)
+        return (
+            pltpu.make_async_copy(old_keys.at[seqs], kf.at[g, :, pl.ds(0, CACHE)], k_sem.at[g, 0]),
+            pltpu.make_async_copy(old_values.at[seqs], vf.at[g, :, pl.ds(0, CACHE)], k_sem.at[g, 1]),
+        )
+
+    late_loads = (
+        pltpu.make_async_copy(master_in, master, m_sem.at[0]),
+        pltpu.make_async_copy(first_in, first_m, m_sem.at[1]),
+        pltpu.make_async_copy(second_in, second_m, m_sem.at[2]),
+    )
+    token_load = pltpu.make_async_copy(tokens_in, xs, m_sem.at[3])
+    token_load.start()
+    for copy in weight_loads:
+        copy.start()
+    for g in range(4):
+        for copy in cache_loads(g):
+            copy.start()
+
     barrier = pltpu.get_barrier_semaphore()
 
     def greet(target):
@@ -93,11 +125,8 @@
         return send(sr.at[0, j], sr.at[1, j], s_send.at[j], s_recv.at[j], across)
 
     def heads_z(dz):
-        return send(heads, ag.at[dz], g_send.at[dz], g_recv.at[dz], device(x, yl, c, (z + dz) % 4, yh))
-
-    @pl.loop(1, 4)
-    def _(dz):
-      heads_z(dz).start()
+        return send(ag.at[0], ag.at[dz], g_send.at[dz], g_recv.at[dz], device(x, yl, c, (z + dz) % 4, yh))
+
 
     for j in range(CHUNKS):
         load(ctx, cb.at[0, j], j, 0).wait()
@@ -105,12 +134,14 @@
             own_up(j).start()
             own_dn(j).start()
         load(outg, sr.at[0, j], j, 1).wait()
-        if j < 2: trade(j).start()
-
-    tot[0] = counts[...]
+        if j < 1: trade(j).start()
+
+    for p in range(8):
+        count = rewards[p, 0] + rewards[p, 1] + rewards[p, 2] + rewards[p, 3]
+        tot[0, p : p + 1, :] = jnp.full((1, LANE), count.astype(F32))
 
     def count_copy(d):
-        return send(counts, tot.at[d], t_send.at[d], t_recv.at[d], {"rep": (rep + d) % 16, "tp": tp})
+        return send(tot.at[0], tot.at[d], t_send.at[d], t_recv.at[d], {"rep": (rep + d) % 16, "tp": tp})
 
     @pl.loop(1, 16)
     def _(d):
@@ -134,6 +165,86 @@
                 ).astype(BF)
 
     scale(0)
+    for copy in late_loads:
+        copy.start()
+
+    def attention():
+        qa[...] = jnp.zeros_like(qa)
+        ka[...] = jnp.zeros_like(ka)
+        va[...] = jnp.zeros_like(va)
+        token_load.wait()
+        for copy in weight_loads:
+            copy.wait()
+
+        @pl.loop(0, 3)
+        def _(n):
+            for base, held in ((0, give), (1536, part)):
+                some = xs[:, pl.ds(pl.multiple_of(base + n * 512, 512), 512)]
+                qa[...] += jnp.dot(some, held[n + 2].reshape(512, 640), preferred_element_type=F32)
+
+        @pl.loop(0, 4)
+        def _(n):
+            some = xs[:, pl.ds(pl.multiple_of(3072 + n * 512, 512), 512)]
+            held = ss[1, pl.ds(pl.multiple_of(n * 512, 512), 512), :]
+            qa[...] += jnp.dot(some, held, preferred_element_type=F32)
+
+        @pl.loop(0, 8)
+        def _(m):
+            some = xs[:, pl.ds(pl.multiple_of(m * 640, 640), 640)]
+            ka[...] += jnp.dot(some, dgive[m // 2, m % 2].reshape(640, LANE), preferred_element_type=F32)
+            va[...] += jnp.dot(some, dpart[m // 2, m % 2].reshape(640, LANE), preferred_element_type=F32)
+
+    def attention_scores():
+        qb[...] = jnp.zeros_like(qb)
+        kn[...] = jnp.zeros_like(kn)
+        vn[...] = jnp.zeros_like(vn)
+
+        def turned(vectors):
+            return vectors * cosine[...] + pltpu.roll(vectors, 64, 1) * sine[...]
+
+        def rounded(vectors):
+            return vectors.astype(BF).astype(F32)
+
+        for h in range(5):
+            turned_query = rounded(turned(qa[:, h * LANE : (h + 1) * LANE]))
+            for t in range(4):
+                qb[:, t * 5 + h, :] = turned_query[t * 32 : (t + 1) * 32]
+        turned_key = rounded(turned(ka[...]))
+        value = rounded(va[...])
+        for t in range(4):
+            kn[:, t, :] = turned_key[t * 32 : (t + 1) * 32]
+            vn[:, t, :] = value[t * 32 : (t + 1) * 32]
+
+        column = lax.broadcasted_iota(jnp.int32, (24, CACHE + 16), 1)
+        row = lax.broadcasted_iota(jnp.int32, (24, CACHE + 16), 0)
+        fresh = jnp.logical_and(
+            jnp.logical_and(column >= CACHE, column < CACHE + 4), (column - CACHE) * 5 <= row
+        )
+
+        @pl.loop(0, 4)
+        def _(g):
+            slot = g
+            for copy in cache_loads(g):
+                copy.wait()
+            live = jnp.logical_or(column < lengths[g], fresh)
+
+            @pl.loop(0, 8)
+            def _(i):
+                s = g * 8 + i
+                kf[slot, i, CACHE : CACHE + 16, :] = kn[s].astype(BF)
+                vf[slot, i, CACHE : CACHE + 16, :] = vn[s].astype(BF)
+                scores = lax.dot_general(
+                    qb[s].astype(BF), kf[slot, i], (((1,), (1,)), ((), ())), preferred_element_type=F32
+                ) * (HEAD_DIM**-0.5)
+                scores = jnp.where(live, scores, -1e30)
+                grown = jnp.exp(scores - jnp.max(scores, axis=-1, keepdims=True))
+                weights = (grown / jnp.sum(grown, axis=-1, keepdims=True)).astype(BF)
+                att[s] = jnp.dot(weights, vf[slot, i], preferred_element_type=F32)
+
+        for h in range(5):
+            for t in range(4):
+                hb[t * 32 : (t + 1) * 32, :] = att[:, t * 5 + h, :]
+            ag[0, h * LANE : (h + 1) * LANE, :] = hb[...].T.astype(BF)
 
     def step(j):
         own_up(j).wait_recv()
@@ -143,8 +254,6 @@
         if j + 2 < CHUNKS:
             own_up(j + 2).start()
             own_dn(j + 2).start()
-        if j + 2 < CHUNKS:
-            trade(j + 2).start()
 
     def far(j):
         fwd_up(j).wait_recv()
@@ -248,7 +357,6 @@
         return (z - dz + 4) % 4 == x
 
     def heads_over_x():
-        ag[0] = heads[...]
         for dz in (1, 2, 3):
             heads_z(dz).wait_recv()
 
@@ -278,15 +386,14 @@
         def _(k):
             pltpu.make_async_copy(hx.at[k], hx.at[k], i_recv.at[k]).wait()
 
-        for h in range(2):
-            for other in range(2):
-                @pl.when(stays(h, other))
-                def _():
-                    spread(h, other, True).start()
-
-                @pl.when(jnp.logical_not(stays(h, other)))
-                def _():
-                    spread(h, other, False).start()
+    def spread_one(h, other):
+        @pl.when(stays(h, other))
+        def _():
+            spread(h, other, True).start()
+
+        @pl.when(jnp.logical_not(stays(h, other)))
+        def _():
+            spread(h, other, False).start()
 
     def take_heads():
         for k in range(4):
@@ -297,13 +404,23 @@
             aa[g] = ab[g // 4, g % 4].T
 
     step(0)
+    trade(1).start()
     contribute(0, 3, (0,))
-    heads_over_x()
     step(1)
+    trade(2).start()
     contribute(4, 7, (0,))
+    attention()
     far(0)
+    trade(3).start()
     contribute(3, 4, (0,))
+    attention_scores()
+
+    @pl.loop(1, 4)
+    def _(dz):
+        heads_z(dz).start()
+
     step(2)
+    trade(4).start()
     contribute(8, 11, (0,))
     far(1)
     contribute(7, 8, (0,))
@@ -311,24 +428,29 @@
     contribute(12, 15, (0,))
     for j in range(CHUNKS):
         trade(j).wait_recv()
-    spread_heads()
     scale(1)
     contribute(0, 11, (1,))
+    heads_over_x()
     far(2)
     contribute(11, 12, (0, 1))
     contribute(12, 15, (1,))
     step(4)
+    spread_heads()
+    spread_one(0, 0)
+    spread_one(0, 1)
     contribute(16, 19, (0, 1))
+    spread_one(1, 0)
+    spread_one(1, 1)
     x_sum(0)
     x_sum(1)
     far(3)
     contribute(15, 16, (0, 1))
     x_sum(2)
-    take_heads()
     far(4)
     contribute(19, 20, (0, 1))
     x_sum(3)
     x_sum(4)
+    take_heads()
 
     for core, sizes, starts in ((0, (128, 128, 64), (0, 128, 256)), (1, (64, 128, 128), (0, 64, 192))):
         @pl.when(c == core)
@@ -337,6 +459,9 @@
                 for k in range(3):
                     there = ob.at[src, pl.ds(starts[k], sizes[k])]
                     pltpu.make_async_copy(there, there, o_recv.at[src, k]).wait()
+
+    for copy in late_loads:
+        copy.wait()
 
     @pl.loop(0, ROWS // 32)
     def _(n):
@@ -513,12 +638,17 @@
               spread(h, other, False).wait_send()
 
 
-def learn_and_decode(context, out_grad, rewards, counts, heads, master, first_moment, second_moment):
+def learn_and_decode(
+    context, out_grad, rewards, lengths, cosine, sine, tokens_in, w_query, w_query_rows, w_key, w_value,
+    old_keys, old_values, master, first_moment, second_moment,
+):
     dma = pltpu.SemaphoreType.DMA
     vmem = pltpu.VMEM
     tokens, width = context.shape
-    grid_all = [pl.BlockSpec(memory_space=pl.ANY)] * 2 + [pl.BlockSpec(memory_space=pltpu.SMEM)]
-    grid_all += [pl.BlockSpec(memory_space=pltpu.VMEM)] * 5
+    anywhere = pl.BlockSpec(memory_space=pl.ANY)
+    in_smem = pl.BlockSpec(memory_space=pltpu.SMEM)
+    in_vmem = pl.BlockSpec(memory_space=pltpu.VMEM)
+    grid_all = [anywhere] * 2 + [in_smem] * 2 + [in_vmem] * 2 + [anywhere] * 10
     return pl.pallas_call(
         step_kernel,
         out_shape=(
@@ -568,58 +698,23 @@
             dma((2, 3)), dma((2, 3)),
             dma((2,)), dma((2,)),
             dma((2, 7)), dma((2, 8)),
+            vmem((LANE, 8 * width), BF),
+            vmem((LANE, width), F32), vmem((LANE, LANE), F32), vmem((LANE, LANE), F32),
+            vmem((32, 24, LANE), F32), vmem((32, 16, LANE), F32), vmem((32, 16, LANE), F32),
+            vmem((4, 8, CACHE + 16, LANE), BF), vmem((4, 8, CACHE + 16, LANE), BF),
+            vmem((32, 24, LANE), F32), vmem((LANE, LANE), F32),
+            vmem((ROWS, width), F32), vmem((ROWS, width), F32), vmem((ROWS, width), F32),
+            dma((5,)), dma((4, 2)), dma((4,)),
         ],
         compiler_params=pltpu.CompilerParams(
-            collective_id=0, has_side_effects=True, vmem_limit_bytes=62 * 1024 * 1024
+            collective_id=0, has_side_effects=True, vmem_limit_bytes=63 * 1024 * 1024
         ),
         cost_estimate=pl.CostEstimate(flops=14_300_000_000, bytes_accessed=10_000_000, transcendentals=0),
         name="learn_and_decode",
-    )(context, out_grad, rewards, counts, heads, master, first_moment, second_moment)
-
-
-def rotate(vectors, positions):
-    half_dim = vectors.shape[-1] // 2
-    frequency = rope_base ** (-2.0 * jnp.arange(half_dim, dtype=jnp.float32) / vectors.shape[-1])
-    angles = positions[..., None].astype(jnp.float32) * frequency
-    cosine_table = jnp.cos(angles)
-    sine_table = jnp.sin(angles)
-    former = vectors[..., :half_dim]
-    latter = vectors[..., half_dim:]
-    return jnp.concatenate(
-        [former * cosine_table - latter * sine_table, latter * cosine_table + former * sine_table],
-        axis=-1,
+    )(
+        context, out_grad, rewards, lengths, cosine, sine, tokens_in, w_query, w_query_rows, w_key, w_value,
+        old_keys, old_values, master, first_moment, second_moment,
     )
-
-
-def attend(queries, old_keys, old_values, new_keys, new_values, live_mask):
-    score_scale = HEAD_DIM ** (-0.5)
-    step_total = queries.shape[0]
-    cache_scores = (
-        jnp.einsum("tsgqd,scgd->tsgqc", queries, old_keys, preferred_element_type=jnp.float32)
-        * score_scale
-    )
-    cache_scores = jnp.where(live_mask[None, :, None, None, :], cache_scores, -1e30)
-    recent = (
-        jnp.einsum("tsgqd,usgd->tsgqu", queries, new_keys, preferred_element_type=jnp.float32)
-        * score_scale
-    )
-    causal = jnp.arange(step_total)[:, None] >= jnp.arange(step_total)[None, :]
-    recent = jnp.where(causal[:, None, None, None, :], recent, -1e30)
-    row_peak = jnp.maximum(jnp.max(cache_scores, axis=-1), jnp.max(recent, axis=-1))[..., None]
-    cache_exp = jnp.exp(cache_scores - row_peak)
-    recent_exp = jnp.exp(recent - row_peak)
-    denominator = jnp.sum(cache_exp, axis=-1, keepdims=True) + jnp.sum(
-        recent_exp, axis=-1, keepdims=True
-    )
-    cache_weight = (cache_exp / denominator).astype(jnp.bfloat16)
-    recent_weight = (recent_exp / denominator).astype(jnp.bfloat16)
-    attended = jnp.einsum(
-        "tsgqc,scgd->tsgqd", cache_weight, old_values, preferred_element_type=jnp.float32
-    )
-    attended = attended + jnp.einsum(
-        "tsgqu,usgd->tsgqd", recent_weight, new_values, preferred_element_type=jnp.float32
-    )
-    return attended.astype(jnp.bfloat16)
 
 
 def per_device(
@@ -637,36 +732,20 @@
     cache_values,
     lengths,
 ):
-    counts = jnp.broadcast_to(
-        jnp.sum(rewards, axis=1).astype(F32)[:, None], (rewards.shape[0], LANE)
-    )
     step_total, seq_local, model_width = inputs.shape
-    local_heads = w_query.shape[1] // HEAD_DIM
-    local_kv = w_key.shape[1] // HEAD_DIM
-    flat_rows = inputs.reshape(step_total * seq_local, model_width)
-    projected = lax.optimization_barrier(jnp.dot(flat_rows, w_query, preferred_element_type=F32))
-    queries = projected.reshape(step_total, seq_local, local_heads, HEAD_DIM)
-    key_new = jnp.dot(flat_rows, w_key, preferred_element_type=F32).reshape(
-        step_total, seq_local, local_kv, HEAD_DIM
-    )
-    value_new = (
-        jnp.dot(flat_rows, w_value, preferred_element_type=F32)
-        .reshape(step_total, seq_local, local_kv, HEAD_DIM)
-        .astype(BF)
-    )
     seq_length = jnp.repeat(lengths, seq_local // lengths.shape[0])
     positions = seq_length[None, :] + jnp.arange(step_total, dtype=jnp.int32)[:, None]
-    queries = rotate(queries, positions[:, :, None]).astype(BF)
-    queries = queries.reshape(step_total, seq_local, local_kv, local_heads // local_kv, HEAD_DIM)
-    key_new = rotate(key_new, positions[:, :, None]).astype(BF)
-    slot_total = cache_keys.shape[1]
-    old_keys = cache_keys.reshape(seq_local, slot_total, local_kv, HEAD_DIM)
-    old_values = cache_values.reshape(seq_local, slot_total, local_kv, HEAD_DIM)
-    live_mask = jnp.arange(slot_total, dtype=jnp.int32)[None, :] < seq_length[:, None]
-    attended = attend(queries, old_keys, old_values, key_new, value_new, live_mask)
-    heads = attended.reshape(step_total * seq_local, local_heads * HEAD_DIM).T
+    half_dim = HEAD_DIM // 2
+    frequency = rope_base ** (-2.0 * jnp.arange(half_dim, dtype=F32) / HEAD_DIM)
+    angles = positions.reshape(-1, 1).astype(F32) * frequency
+    cosine = jnp.concatenate([jnp.cos(angles), jnp.cos(angles)], axis=1)
+    sine = jnp.concatenate([-jnp.sin(angles), jnp.sin(angles)], axis=1)
     adam_step, decoded = learn_and_decode(
-        context, out_grad, rewards, counts, heads, master, first_moment, second_moment
+        context, out_grad, rewards, lengths, cosine, sine,
+        inputs.reshape(step_total * seq_local, model_width),
+        w_query.reshape(10, 4, LANE, 5 * LANE), w_query,
+        w_key.reshape(4, 2, CHUNKS, LANE, LANE), w_value.reshape(4, 2, CHUNKS, LANE, LANE),
+        cache_keys, cache_values, master, first_moment, second_moment,
     )
     return (decoded.reshape(step_total, seq_local, model_width), adam_step)
 

time: 194 us -> 186 us (0.959)
  matrix products: 9.63 us -> 0 us
  Pallas kernels: 171 us -> 179 us
  local copies, waits for them, and re-layouts: 8.87 us -> 5.67 us
    dot_general x7 -> x0, matrix products: 9.63 us -> none  [the longest x1 4.06 us: per_device(): jnp.dot(flat_rows, w_query, preferred_element_type=F32)]
    pallas_call x1, Pallas kernels: 171 us -> 179 us  [learn_and_decode(): pl.pallas_call(step_kernel, out_shape=(jax.ShapeDtypeStruct((ROWS, width)...]
    unnamed x14 -> x5, local copies, waits for them, and re-layouts: 6.2 us -> 4.78 us
where the time goes in v3:
time: 186 us
  Pallas kernels  179 us (96%)
  local copies, waits for them, and re-layouts  5.67 us (3%)
    pallas_call x1, Pallas kernels, learn_and_decode(): pl.pallas_call(step_kernel, out_shape=(jax.ShapeDtypeStruct((ROWS, width)...  179 us
    unnamed x5, local copies, waits for them, and re-layouts  4.78 us

profile of v3, /device:TPU:0, one launch (start us, length us, event | category | flops | bytes accessed | tf_op | source)
XLA Modules:
  0.0 186.1 jit_solution(7754421754057278605)
XLA Ops:
  0.6 0.7 broadcast_in_dim.2
  1.4 0.1 add.21
  1.5 0.1 convert_element_type.12
  1.6 1.4 copy.15.rewards
  2.9 0.3 fusion
  3.2 0.8 pad_maximum_fusion
  4.0 178.7 %learn_and_decode.1 = (f32[320,640]{1,0:T(8,128)}, bf16[128,5120]{1,0:T(8,128)(2,1)}) custom-call(bf16[2048,640]{1,0:T(8,128)(2,1)} %ctx.1, bf16[2048,640]{1,0:T(8,128)(2,1)} %outg.1, s32[8,4]{1,0:T(8,128)} %copy.15.rewards, s32[4]{0:T(128)} %lengths.1, f32[128,128]{1,0:T(8,128)} %get-tuple-element.9.cosine, f32[128,128]{1,0:T(8,128)} %get-tuple-element.10.sine, ...), custom_call_target="tpu_custom_call" | custom-call | flops 14300000256 | bytes 10000000 | tf_op jit(solution)/shard_map/learn_and_decode/pallas_call | solution.py:652
  182.7 0.0 copy-start
  182.7 2.5 %copy.18 = bf16[4,32,5120]{2,1,0:T(8,128)(2,1)} copy(bf16[4,32,5120]{2,1,0:T(8,128)(2,1)} %bitcast.5) | data formatting | bytes 2621440
  185.2 0.0 copy-done
  185.2 0.9 copy.19
  (2 shorter events, 0.0 us)
Async XLA Ops:
  182.7 2.5 %copy-start = (f32[320,640]{1,0:T(8,128)S(1)}, f32[320,640]{1,0:T(8,128)}, u32[]{:S(2)}) copy-start(f32[320,640]{1,0:T(8,128)} %get-tuple-element.14) | copy-start | bytes 2457604

commit v4 on v3

--- a/solution.py
+++ b/solution.py
@@ -424,33 +424,33 @@
     contribute(8, 11, (0,))
     far(1)
     contribute(7, 8, (0,))
+    heads_over_x()
     step(3)
     contribute(12, 15, (0,))
     for j in range(CHUNKS):
         trade(j).wait_recv()
-    scale(1)
-    contribute(0, 11, (1,))
-    heads_over_x()
-    far(2)
-    contribute(11, 12, (0, 1))
-    contribute(12, 15, (1,))
-    step(4)
     spread_heads()
     spread_one(0, 0)
     spread_one(0, 1)
-    contribute(16, 19, (0, 1))
+    scale(1)
+    contribute(0, 11, (1,))
+    far(2)
+    contribute(11, 12, (0, 1))
     spread_one(1, 0)
     spread_one(1, 1)
+    step(4)
+    contribute(12, 15, (1,))
+    contribute(16, 19, (0, 1))
     x_sum(0)
-    x_sum(1)
     far(3)
     contribute(15, 16, (0, 1))
-    x_sum(2)
+    x_sum(1)
     far(4)
     contribute(19, 20, (0, 1))
+    take_heads()
+    x_sum(2)
     x_sum(3)
     x_sum(4)
-    take_heads()
 
     for core, sizes, starts in ((0, (128, 128, 64), (0, 128, 256)), (1, (64, 128, 128), (0, 64, 192))):
         @pl.when(c == core)
@@ -569,19 +569,19 @@
         for dz in (2, 1, 3):
             d_over_z(q, dz, 1).start()
 
-    d_multiply(0)
-    if len(SPANS) > 1:
-        d_multiply(1)
-    d_x_sum(0)
-    if len(SPANS) > 1:
-        for dx in (2, 1, 3):
-            d_over_x(1, dx).start()
-    d_finish(0)
-    d_pass(0)
-    if len(SPANS) > 1:
-        d_x_sum(1)
-        d_finish(1)
-        d_pass(1)
+    parts = len(SPANS)
+    for q in range(parts):
+        d_multiply(q)
+    for q in range(parts + 1):
+        if q < parts:
+            d_x_sum(q)
+        if q + 1 < parts:
+            for dx in (2, 1, 3):
+                d_over_x(q + 1, dx).start()
+        if q > 0:
+            d_pass(q - 1)
+        if q < parts:
+            d_finish(q)
 
     for q in range(len(SPANS)):
         start, width = SPANS[q]
@@ -694,10 +694,10 @@
             dma((4,)), dma((4,)),
             dma((4,)), dma((4,)),
             dma((2, 2)), dma((4,)),
-            dma((2, 4)), dma((2, 4)),
-            dma((2, 3)), dma((2, 3)),
-            dma((2,)), dma((2,)),
-            dma((2, 7)), dma((2, 8)),
+            dma((3, 4)), dma((3, 4)),
+            dma((3, 3)), dma((3, 3)),
+            dma((3,)), dma((3,)),
+            dma((3, 7)), dma((3, 8)),
             vmem((LANE, 8 * width), BF),
             vmem((LANE, width), F32), vmem((LANE, LANE), F32), vmem((LANE, LANE), F32),
             vmem((32, 24, LANE), F32), vmem((32, 16, LANE), F32), vmem((32, 16, LANE), F32),

time: 186 us -> 176 us (0.946)
  Pallas kernels: 179 us -> 168 us
    pallas_call x1, Pallas kernels: 179 us -> 168 us  [learn_and_decode(): pl.pallas_call(step_kernel, out_shape=(jax.ShapeDtypeStruct((ROWS, width)...]
where the time goes in v4:
time: 176 us
  Pallas kernels  168 us (95%)
  local copies, waits for them, and re-layouts  5.67 us (3%)
    pallas_call x1, Pallas kernels, learn_and_decode(): pl.pallas_call(step_kernel, out_shape=(jax.ShapeDtypeStruct((ROWS, width)...  168 us
    unnamed x5, local copies, waits for them, and re-layouts  4.78 us

profile of v4, /device:TPU:0, one launch (start us, length us, event | category | flops | bytes accessed | tf_op | source)
XLA Modules:
  0.0 175.8 jit_solution(12286825626203916111)
XLA Ops:
  0.6 0.7 broadcast_in_dim.2
  1.4 0.1 add.21
  1.5 0.1 convert_element_type.12
  1.6 1.4 copy.15.rewards
  2.9 0.3 fusion
  3.2 0.8 pad_maximum_fusion
  4.0 168.4 %learn_and_decode.1 = (f32[320,640]{1,0:T(8,128)}, bf16[128,5120]{1,0:T(8,128)(2,1)}) custom-call(bf16[2048,640]{1,0:T(8,128)(2,1)} %ctx.1, bf16[2048,640]{1,0:T(8,128)(2,1)} %outg.1, s32[8,4]{1,0:T(8,128)} %copy.15.rewards, s32[4]{0:T(128)} %lengths.1, f32[128,128]{1,0:T(8,128)} %get-tuple-element.9.cosine, f32[128,128]{1,0:T(8,128)} %get-tuple-element.10.sine, ...), custom_call_target="tpu_custom_call" | custom-call | flops 14300000256 | bytes 10000000 | tf_op jit(solution)/shard_map/learn_and_decode/pallas_call | solution.py:652
  172.3 0.0 copy-start
  172.4 2.5 %copy.18 = bf16[4,32,5120]{2,1,0:T(8,128)(2,1)} copy(bf16[4,32,5120]{2,1,0:T(8,128)(2,1)} %bitcast.5) | data formatting | bytes 2621440
  174.9 0.0 copy-done
  174.9 0.9 copy.19
  (2 shorter events, 0.0 us)
Async XLA Ops:
  172.3 2.5 %copy-start = (f32[320,640]{1,0:T(8,128)S(1)}, f32[320,640]{1,0:T(8,128)}, u32[]{:S(2)}) copy-start(f32[320,640]{1,0:T(8,128)} %get-tuple-element.14) | copy-start | bytes 2457604
